TPU v7x, 8 devices: a whole 2x2x1 slice. The times are simulated.
8 devices in a mesh: data: 1 (over z), expert: 8 (over y, x, core).
Axes of the slice: x: 2, y: 2, z: 1, core: 2. Of those that a mesh axis runs over, the one named last changes fastest.
Arguments:
- x_a: bfloat16 [8192, 1024], P(('data', 'expert'))
- x_b: bfloat16 [8192, 1024], P(('data', 'expert'))
- dy_b: bfloat16 [8192, 1024], P(('data', 'expert'))
- eid_a: int32 [8192, 8], P(('data', 'expert'))
- slot_a: int32 [8192, 8], P(('data', 'expert'))
- gate_a: bfloat16 [8192, 8], P(('data', 'expert'))
- eid_b: int32 [8192, 8], P(('data', 'expert'))
- slot_b: int32 [8192, 8], P(('data', 'expert'))
- gate_b: bfloat16 [8192, 8], P(('data', 'expert'))
- u_b: bfloat16 [32, 4096, 1024], P(('data', 'expert'))
- norm_1: bfloat16 [1024], replicated
- norm_2: bfloat16 [1024], replicated
- w_q: bfloat16 [1024, 16, 64], replicated
- w_k: bfloat16 [1024, 8, 64], replicated
- w_v: bfloat16 [1024, 8, 64], replicated
- w_o: bfloat16 [16, 64, 1024], replicated
- w_1: bfloat16 [32, 1024, 512], P('expert')
- w_2: bfloat16 [32, 512, 1024], P('expert')
- w_3: bfloat16 [32, 1024, 512], P('expert')
Outputs:
- output 1: bfloat16 [8192, 1024], P(('data', 'expert'))
- output 2: bfloat16 [8192, 1024], P(('data', 'expert'))
- output 3: float32 [32, 1024, 512], P(('data', 'expert'))
- output 4: float32 [32, 512, 1024], P(('data', 'expert'))
- output 5: float32 [32, 1024, 512], P(('data', 'expert'))
- output 6: float32 [8, 1024, 16, 64], P(('data', 'expert'))
- output 7: float32 [8, 1024, 8, 64], P(('data', 'expert'))
- output 8: float32 [8, 1024, 8, 64], P(('data', 'expert'))
- output 9: float32 [8, 16, 64, 1024], P(('data', 'expert'))
- output 10: float32 [8, 1024], P(('data', 'expert'))
- output 11: float32 [8, 1024], P(('data', 'expert'))
All inputs are finite; a program needn't handle non-finite values.
Results may differ from a plain program's by a relative error of at most 0.018046.
Values are sent between devices in bfloat16 or wider.
A program may use at most 1 GiB of HBM per device.

v0:
```python
import jax
import jax.numpy as jnp
from jax import lax
from jax.sharding import PartitionSpec as P

NORM_EPS = 1e-6


def rms_norm(values, gain):
    wide = values.astype(jnp.float32)
    scaled = wide * lax.rsqrt(jnp.mean(wide * wide, axis=-1, keepdims=True) + NORM_EPS)
    return (scaled * gain.astype(jnp.float32)).astype(jnp.bfloat16)


def add_rows(first, second):
    return (first.astype(jnp.float32) + second.astype(jnp.float32)).astype(jnp.bfloat16)


def attn_out(x_rows, norm_gain, w_q, w_k, w_v, w_o):
    tokens = x_rows.shape[0]
    heads = w_q.shape[1]
    kv_heads = w_k.shape[1]
    head_dim = w_q.shape[2]
    normed = rms_norm(x_rows, norm_gain)
    query = jnp.einsum('td,dhe->the', normed, w_q, preferred_element_type=jnp.float32).astype(jnp.bfloat16)
    query = query.reshape(tokens, kv_heads, heads // kv_heads, head_dim)
    key_proj = jnp.einsum('td,dge->tge', normed, w_k, preferred_element_type=jnp.float32).astype(jnp.bfloat16)
    val_proj = jnp.einsum('td,dge->tge', normed, w_v, preferred_element_type=jnp.float32).astype(jnp.bfloat16)
    scores = jnp.einsum('tgre,mge->grtm', query, key_proj, preferred_element_type=jnp.float32) * head_dim ** -0.5
    causal = jnp.arange(tokens)[:, None] >= jnp.arange(tokens)[None, :]
    scores = jnp.where(causal, scores, -1e30)
    probs = jax.nn.softmax(scores, axis=-1).astype(jnp.bfloat16)
    context = jnp.einsum('grtm,mge->tgre', probs, val_proj, preferred_element_type=jnp.float32).astype(jnp.bfloat16)
    context = context.reshape(tokens, heads, head_dim)
    return jnp.einsum('the,hed->td', context, w_o, preferred_element_type=jnp.float32).astype(jnp.bfloat16)


def dispatch(row_vals, expert_ids, slot_ids, experts, capacity):
    safe_slots = jnp.where(slot_ids >= 0, slot_ids, capacity)
    values = jnp.broadcast_to(row_vals, expert_ids.shape + (row_vals.shape[-1],))
    return jnp.zeros((experts, capacity, row_vals.shape[-1]), jnp.bfloat16).at[expert_ids, safe_slots].set(values, mode='drop')


def pick_rows(buf, expert_ids, slot_ids):
    safe_slots = jnp.where(slot_ids >= 0, slot_ids, buf.shape[1])
    return buf.at[expert_ids, safe_slots].get(mode='fill', fill_value=0)


def device_backward(x_dev, dy_dev, du_dev, norm_1, norm_2, w_q, w_k, w_v, w_o):
    attn_val, attn_pull = jax.vjp(attn_out, x_dev, norm_1, w_q, w_k, w_v, w_o)
    h_dev = add_rows(x_dev, attn_val)
    _, norm_pull = jax.vjp(rms_norm, h_dev, norm_2)
    dh_norm, grad_n2 = norm_pull(du_dev)
    dh_dev = add_rows(dy_dev, dh_norm)
    grad_x, grad_n1, grad_q, grad_k, grad_v, grad_o = attn_pull(dh_dev)
    return (add_rows(dh_dev, grad_x), grad_q.astype(jnp.float32), grad_k.astype(jnp.float32), grad_v.astype(jnp.float32), grad_o.astype(jnp.float32), grad_n1.astype(jnp.float32), grad_n2.astype(jnp.float32))


def solution(mesh):
    group = mesh.shape['expert']

    def local_step(x_a, x_b, dy_b, eid_a, slot_a, gate_a, eid_b, slot_b, gate_b, u_b, norm_1, norm_2, w_q, w_k, w_v, w_o, w_1, w_2, w_3):
        local_experts = w_1.shape[0]
        experts = local_experts * group
        capacity = u_b.shape[1] // group
        model_dim = x_a.shape[1]

        h_a = add_rows(x_a, attn_out(x_a, norm_1, w_q, w_k, w_v, w_o))
        u_a = rms_norm(h_a, norm_2)
        send_a = dispatch(u_a[:, None, :], eid_a, slot_a, experts, capacity).reshape(group, local_experts, capacity, model_dim)
        recv_a = lax.all_to_all(send_a, 'expert', 0, 0, tiled=True)
        act_1 = jnp.einsum('pecd,edf->pecf', recv_a, w_1, preferred_element_type=jnp.float32).astype(jnp.bfloat16).astype(jnp.float32)
        act_3 = jnp.einsum('pecd,edf->pecf', recv_a, w_3, preferred_element_type=jnp.float32).astype(jnp.bfloat16).astype(jnp.float32)
        hidden = (act_1 * jax.nn.sigmoid(act_1) * act_3).astype(jnp.bfloat16)
        out_a = jnp.einsum('pecf,efd->pecd', hidden, w_2, preferred_element_type=jnp.float32).astype(jnp.bfloat16)
        back_a = lax.all_to_all(out_a, 'expert', 0, 0, tiled=True).reshape(experts, capacity, model_dim)
        mixed = jnp.einsum('tk,tkd->td', gate_a, pick_rows(back_a, eid_a, slot_a), preferred_element_type=jnp.float32)
        y_a = (h_a.astype(jnp.float32) + mixed).astype(jnp.bfloat16)

        grad_rows = gate_b[:, :, None] * dy_b[:, None, :]
        send_b = dispatch(grad_rows, eid_b, slot_b, experts, capacity).reshape(group, local_experts, capacity, model_dim)
        d_out = lax.all_to_all(send_b, 'expert', 0, 0, tiled=True)
        saved = u_b.reshape(local_experts, group, capacity, model_dim)
        pre_1 = jnp.einsum('epcd,edf->pecf', saved, w_1, preferred_element_type=jnp.float32).astype(jnp.bfloat16).astype(jnp.float32)
        pre_3 = jnp.einsum('epcd,edf->pecf', saved, w_3, preferred_element_type=jnp.float32).astype(jnp.bfloat16).astype(jnp.float32)
        sigma = jax.nn.sigmoid(pre_1)
        silu_1 = pre_1 * sigma
        hid_b = (silu_1 * pre_3).astype(jnp.bfloat16)
        grad_w2 = jnp.einsum('pecf,pecd->efd', hid_b, d_out, preferred_element_type=jnp.float32)
        grad_hid = jnp.einsum('pecd,efd->pecf', d_out, w_2, preferred_element_type=jnp.float32).astype(jnp.bfloat16).astype(jnp.float32)
        grad_a1 = (grad_hid * pre_3 * sigma * (1.0 + pre_1 * (1.0 - sigma))).astype(jnp.bfloat16)
        grad_a3 = (grad_hid * silu_1).astype(jnp.bfloat16)
        grad_w1 = jnp.einsum('epcd,pecf->edf', saved, grad_a1, preferred_element_type=jnp.float32)
        grad_w3 = jnp.einsum('epcd,pecf->edf', saved, grad_a3, preferred_element_type=jnp.float32)
        grad_in = (jnp.einsum('pecf,edf->pecd', grad_a1, w_1, preferred_element_type=jnp.float32) + jnp.einsum('pecf,edf->pecd', grad_a3, w_3, preferred_element_type=jnp.float32)).astype(jnp.bfloat16)
        back_b = lax.all_to_all(grad_in, 'expert', 0, 0, tiled=True).reshape(experts, capacity, model_dim)
        du_rows = jnp.sum(pick_rows(back_b, eid_b, slot_b), axis=1, dtype=jnp.float32).astype(jnp.bfloat16)
        dx_b, g_q, g_k, g_v, g_o, g_n1, g_n2 = device_backward(x_b, dy_b, du_rows, norm_1, norm_2, w_q, w_k, w_v, w_o)
        return (y_a, dx_b, grad_w1, grad_w2, grad_w3, g_q[None], g_k[None], g_v[None], g_o[None], g_n1[None], g_n2[None])

    row_spec = P(('data', 'expert'), None)
    cube_spec = P(('data', 'expert'), None, None)
    quad_spec = P(('data', 'expert'), None, None, None)
    expert_spec = P('expert', None, None)
    in_specs = (row_spec, row_spec, row_spec, row_spec, row_spec, row_spec, row_spec, row_spec, row_spec, cube_spec, P(), P(), P(), P(), P(), P(), expert_spec, expert_spec, expert_spec)
    out_specs = (row_spec, row_spec, cube_spec, cube_spec, cube_spec, quad_spec, quad_spec, quad_spec, quad_spec, row_spec, row_spec)
    return jax.shard_map(local_step, mesh=mesh, in_specs=in_specs, out_specs=out_specs, check_vma=False)
```

profile of v0, /device:TPU:0, one launch (start us, length us, event | category | flops | bytes accessed | tf_op | source)
XLA Modules:
  0.0 2427.5 jit_solution(4593915899753181189)
XLA Ops:
  8.0 5.9 sort.1
  14.0 9.0 multiply_bitcast_fusion
  22.9 132.0 %scatter_custom_fusion.1 = bf16[16384,1024]{1,0:T(8,128)(2,1)} fusion(s32[8192]{0:T(1024)S(1)} %get-tuple-element.46, bf16[8192,1024]{1,0:T(8,128)(2,1)} %multiply_bitcast_fusion, s32[8192]{0:T(1024)S(1)} %broadcast_clamp_fusion, bf16[]{:T(256)} %constant.40.clone.1), kind=kCustom, calls=%fused_computation.64 | custom fusion | bytes 33554944
  154.9 6.2 all-to-all-start.2
  180.9 33.4 %fusion.166 = (f32[8,2,1024]{2,1,0:T(2,128)}, f32[8,2,1024,1024]{2,3,1,0:T(8,128)}) fusion(pred[1024,1024]{0,1:T(8,128)(4,1)S(1)} %iota_compare_fusion.1, bf16[1024,8,2,64]{0,3,2,1:T(8,128)(2,1)} %bitcast.416, f32[1024,8,64]{0,2,1:T(8,128)} %bitcast.415), kind=kOutput, calls=%fused_computation.228 | convolution fusion | flops 2215117824 | bytes 72417280 | tf_op jit(solution)/shard_map/sub | solution.py:32
  214.3 25.6 %convolution_convert_fusion.2 = bf16[4,512,8,512]{1,3,2,0:T(8,128)(2,1)} fusion(bf16[4,8,512,1024]{3,2,1,0:T(8,128)(2,1)} %bitcast.405, bf16[4,1024,512]{2,1,0:T(8,128)(2,1)} %param.37), kind=kOutput, calls=%fused_computation.79 | convolution fusion | flops 17188257792 | bytes 54525952 | tf_op jit(solution)/shard_map/epcd,edf->pecf/dot_general | solution.py:85
  239.9 286.2 %all-to-all-done.2 = bf16[8,4,512,1024]{3,2,1,0:T(8,128)(2,1)} async-done(((bf16[8,4,512,1024]{3,2,1,0:T(8,128)(2,1)}), bf16[8,4,512,1024]{3,2,1,0:T(8,128)(2,1)}, u32[]{:S(2)}, u32[]{:S(2)}) %all-to-all-start.2) | async-done | bytes 33554464 | tf_op jit(solution)/shard_map/all_to_all | solution.py:82
  526.1 25.1 %fusion.59 = bf16[4,8,512,512]{3,2,1,0:T(8,128)(2,1)} fusion(bf16[8,4,512,1024]{3,2,1,0:T(8,128)(2,1)} %all-to-all-done.2, bf16[4,512,1024]{2,1,0:T(8,128)(2,1)} %param.36), kind=kOutput, calls=%fused_computation.77 | convolution fusion | flops 17188257792 | bytes 54525952 | tf_op jit(solution)/shard_map/pecd,efd->pecf/dot_general | solution.py:90
  551.3 41.2 %fusion.19 = (bf16[8,4,512,512]{3,2,0,1:T(8,128)(2,1)}, bf16[4,512,8,512]{1,3,2,0:T(8,128)(2,1)}) fusion(bf16[4,512,8,512]{1,3,2,0:T(8,128)(2,1)} %convolution_convert_fusion.2, bf16[4,8,512,512]{3,2,1,0:T(8,128)(2,1)} %fusion.59, bf16[4,8,512,1024]{3,2,1,0:T(8,128)(2,1)} %bitcast.406, bf16[4,1024,512]{2,1,0:T(8,128)(2,1)} %param.35), kind=kOutput, calls=%fused_computation.35 | convolution fusion | flops 17297309696 | bytes 104857600 | tf_op jit(solution)/shard_map/epcd,edf->pecf/dot_general | solution.py:84
  592.4 32.7 %fusion.90 = f32[4,8,512,1024]{3,2,1,0:T(8,128)} fusion(bf16[8,4,512,512]{3,2,0,1:T(8,128)(2,1)} %get-tuple-element.64, bf16[4,1024,512]{2,1,0:T(8,128)(2,1)} %param.35), kind=kOutput, calls=%fused_computation.132 | convolution fusion | flops 17179869184 | bytes 88080384 | tf_op jit(solution)/shard_map/pecf,edf->pecd/dot_general | solution.py:95
  625.2 45.1 %fusion.13 = bf16[8,4,512,1024]{3,2,0,1:T(8,128)(2,1)} fusion(f32[4,8,512,1024]{3,2,1,0:T(8,128)} %fusion.90, bf16[4,1024,512]{2,1,0:T(8,128)(2,1)} %param.37, bf16[4,8,512,512]{3,2,1,0:T(8,128)(2,1)} %fusion.59, bf16[4,512,8,512]{1,3,2,0:T(8,128)(2,1)} %get-tuple-element.65), kind=kOutput, calls=%fused_computation.26 | convolution fusion | flops 17280532480 | bytes 138412032 | tf_op jit(solution)/shard_map/pecf,edf->pecd/dot_general | solution.py:95
  670.3 22.8 copy.119
  693.0 6.2 all-to-all-start.3
  710.4 6.6 sort
  730.9 24.5 %fusion.104 = bf16[8,64,2,1024]{3,1,2,0:T(8,128)(2,1)} fusion(f32[8,2,1024,1024]{2,3,1,0:T(8,128)} %get-tuple-element.69, f32[8,2,1024]{2,1,0:T(2,128)S(1)} %copy-done.57, f32[1024,8,64]{0,2,1:T(8,128)} %bitcast.413), kind=kOutput, calls=%fused_computation.154 | convolution fusion | flops 2182610944 | bytes 71368704 | tf_op jit(solution)/shard_map/grtm,mge->tgre/dot_general | solution.py:33
  755.4 6.5 fusion.74
  761.9 23.7 fusion.10
  785.6 21.6 fusion.12
  807.3 34.0 %divide_convert_fusion = bf16[8,2,1024,1024]{2,3,1,0:T(8,128)(2,1)} fusion(f32[8,1024,1024,2]{2,1,3,0:T(8,128)} %get-tuple-element.63, f32[8,2,1024]{2,1,0:T(2,128)S(1)} %fusion.12, f32[8,2,1024]{2,1,0:T(2,128)S(1)} %get-tuple-element.62, pred[1024,1024]{0,1:T(8,128)(4,1)S(1)} %copy-done.8), kind=kLoop, calls=%fused_computation.18 | loop fusion | flops 83886080 | bytes 101842944 | tf_op jit(solution)/shard_map/jvp()/convert_element_type | solution.py:32
  841.3 18.4 convolution_convert_fusion.4
  859.7 6.9 fusion.80
  867.2 195.9 %all-to-all-done.3 = bf16[8,4,512,1024]{3,2,1,0:T(8,128)(2,1)} async-done(((bf16[8,4,512,1024]{3,2,1,0:T(8,128)(2,1)}), bf16[8,4,512,1024]{3,2,1,0:T(8,128)(2,1)}, u32[]{:S(2)}, u32[]{:S(2)}) %all-to-all-start.3) | async-done | bytes 33554464 | tf_op jit(solution)/shard_map/all_to_all | solution.py:96
  1063.1 161.7 %gather_fusion.1 = bf16[8192,1024]{1,0:T(8,128)(2,1)} fusion(bf16[32,512,1024]{2,1,0:T(8,128)(2,1)} %bitcast.44, s32[8192]{0:T(1024)S(1)} %copy-done.2), kind=kCustom, calls=%fused_computation.1 | custom fusion | bytes 33619968 | tf_op jit(solution)/shard_map/gather | solution.py:46
  1224.8 14.5 fusion.49
  1248.1 5.6 add_convert_fusion.2
  1257.6 9.1 broadcast_bitcast_fusion
  1266.7 132.0 %scatter_custom_fusion = bf16[16384,1024]{1,0:T(8,128)(2,1)} fusion(s32[8192]{0:T(1024)} %get-tuple-element.44, bf16[8192,1024]{1,0:T(8,128)(2,1)} %broadcast_bitcast_fusion, s32[8192]{0:T(1024)S(1)} %broadcast_clamp_fusion.1, bf16[]{:T(256)} %constant.40.clone.1), kind=kCustom, calls=%fused_computation.66 | custom fusion | bytes 33554944
  1398.7 6.2 all-to-all-start
  1404.9 28.0 %convolution_bitcast_fusion.1 = f32[4,1024,512]{1,2,0:T(8,128)} fusion(bf16[8,4,512,512]{3,2,0,1:T(8,128)(2,1)} %get-tuple-element.64, bf16[4,8,512,1024]{3,2,1,0:T(8,128)(2,1)} %bitcast.407), kind=kOutput, calls=%fused_computation.144 | convolution fusion | flops 17179869184 | bytes 58720256 | tf_op jit(solution)/shard_map/epcd,pecf->edf/dot_general | solution.py:93
  1433.0 8.7 copy.142
  1441.6 30.1 %convolution_bitcast_fusion = f32[4,1024,512]{1,2,0:T(8,128)} fusion(bf16[4,8,512,1024]{3,2,1,0:T(8,128)(2,1)} %bitcast.408, bf16[4,8,512,512]{3,2,1,0:T(8,128)(2,1)} %fusion.59, bf16[4,512,8,512]{1,3,2,0:T(8,128)(2,1)} %get-tuple-element.65), kind=kOutput, calls=%fused_computation.143 | convolution fusion | flops 17246978048 | bytes 75497472 | tf_op jit(solution)/shard_map/epcd,pecf->edf/dot_general | solution.py:94
  1471.7 8.7 copy.143
  1480.4 29.4 %fusion.95 = f32[4,512,1024]{2,1,0:T(8,128)} fusion(bf16[8,4,512,1024]{3,2,1,0:T(8,128)(2,1)} %all-to-all-done.2, bf16[4,512,8,512]{1,3,2,0:T(8,128)(2,1)} %convolution_convert_fusion.2, bf16[4,512,8,512]{1,3,2,0:T(8,128)(2,1)} %get-tuple-element.65), kind=kOutput, calls=%fused_computation.142 | convolution fusion | flops 17246978048 | bytes 75497472 | tf_op jit(solution)/shard_map/pecf,pecd->efd/dot_general | solution.py:89
  1509.7 259.1 %all-to-all-done = bf16[8,4,512,1024]{3,2,1,0:T(8,128)(2,1)} async-done(((bf16[8,4,512,1024]{3,2,1,0:T(8,128)(2,1)}), bf16[8,4,512,1024]{3,2,1,0:T(8,128)(2,1)}, u32[]{:S(2)}, u32[]{:S(2)}) %all-to-all-start) | async-done | bytes 33554464 | tf_op jit(solution)/shard_map/all_to_all | solution.py:71
  1768.8 26.3 %fusion.37 = bf16[4,8,512,512]{3,2,1,0:T(8,128)(2,1)} fusion(bf16[8,4,512,1024]{3,2,1,0:T(8,128)(2,1)} %all-to-all-done, bf16[4,1024,512]{2,1,0:T(8,128)(2,1)} %param.35), kind=kOutput, calls=%fused_computation.61 | convolution fusion | flops 17179869184 | bytes 54525952 | tf_op jit(solution)/shard_map/pecd,edf->pecf/dot_general | solution.py:72
  1795.1 44.8 %convert_bitcast_fusion.1 = bf16[8,4,512,1024]{3,2,0,1:T(8,128)(2,1)} fusion(bf16[8,4,512,1024]{3,2,1,0:T(8,128)(2,1)} %all-to-all-done, bf16[4,8,512,512]{3,2,1,0:T(8,128)(2,1)} %fusion.37, bf16[4,1024,512]{2,1,0:T(8,128)(2,1)} %param.37, bf16[4,512,1024]{2,1,0:T(8,128)(2,1)} %param.36), kind=kOutput, calls=%fused_computation.50 | convolution fusion | flops 34452013056 | bytes 92274688 | tf_op jit(solution)/shard_map/pecf,efd->pecd/dot_general | solution.py:75
  1839.9 22.7 copy.108
  1862.6 6.0 all-to-all-start.1
  1874.1 39.9 %fusion.9 = (f32[8,2,1024]{2,1,0:T(2,128)S(1)}, bf16[8,2,1024,1024]{2,3,1,0:T(8,128)(2,1)}) fusion(f32[8,1024,1024,2]{2,1,3,0:T(8,128)} %get-tuple-element.63, f32[8,2,1024]{2,1,0:T(2,128)S(1)} %copy-done.36, f32[8,2,1024]{2,1,0:T(2,128)S(1)} %copy-done.26, pred[1024,1024]{0,1:T(8,128)(4,1)S(1)} %copy-done.9, bf16[8,64,2,1024]{3,1,2,0:T(8,128)(2,1)S(1)} %bitcast.395, ...), kind=kOutput, calls=%fused_computation.15 | convolution fusion | flops 2282209280 | bytes 106102784 | tf_op jit(solution)/shard_map/transpose(jvp(grtm,mge->tgre))/dot_general | solution.py:33
  1914.1 44.3 %fusion.7 = bf16[8,1024,1024,2]{2,1,3,0:T(8,128)(2,1)} fusion(bf16[8,2,1024,1024]{2,3,1,0:T(8,128)(2,1)} %get-tuple-element.73, f32[8,1024,1024,2]{2,1,3,0:T(8,128)} %get-tuple-element.63, f32[8,1024,2]{1,2,0:T(2,128)S(1)} %bitcast.402, f32[8,1024,2]{1,2,0:T(2,128)S(1)} %negate_bitcast_fusion, f32[8,1024,2]{1,2,0:T(2,128)S(1)} %bitcast.401, ...), kind=kLoop, calls=%fused_computation.13 | loop fusion | flops 167772160 | bytes 135462912 | tf_op jit(solution)/shard_map/transpose(jvp())/mul | solution.py:29
  1958.4 16.8 bitcast_convert_fusion.7
  1979.1 14.9 convolution_convert_fusion.3
  1999.3 17.6 bitcast_convert_fusion.8
  2016.9 6.2 fusion.69
  2050.4 182.1 %all-to-all-done.1 = bf16[8,4,512,1024]{3,2,1,0:T(8,128)(2,1)} async-done(((bf16[8,4,512,1024]{3,2,1,0:T(8,128)(2,1)}), bf16[8,4,512,1024]{3,2,1,0:T(8,128)(2,1)}, u32[]{:S(2)}, u32[]{:S(2)}) %all-to-all-start.1) | async-done | bytes 33554464 | tf_op jit(solution)/shard_map/all_to_all | solution.py:76
  2232.6 161.6 %gather_fusion = bf16[8192,1024]{1,0:T(8,128)(2,1)} fusion(bf16[32,512,1024]{2,1,0:T(8,128)(2,1)} %bitcast.28, s32[8192]{0:T(1024)S(1)} %copy-done.1), kind=kCustom, calls=%fused_computation | custom fusion | bytes 33619968 | tf_op jit(solution)/shard_map/gather | solution.py:46
  2394.2 18.6 multiply_reduce_fusion
  2412.8 5.4 copy.156
  (182 shorter events, 116.3 us)
Async XLA Ops:
  0.6 176.5 %copy-start = (bf16[1024,16,64]{0,2,1:T(8,128)(2,1)S(1)}, bf16[1024,16,64]{0,2,1:T(8,128)(2,1)}, u32[]{:S(2)}) copy-start(bf16[1024,16,64]{0,2,1:T(8,128)(2,1)} %param.31) | copy-start | bytes 6291460
  154.9 6.2 copy-start.52
  154.9 371.2 %all-to-all-start.2 = ((bf16[8,4,512,1024]{3,2,1,0:T(8,128)(2,1)}), bf16[8,4,512,1024]{3,2,1,0:T(8,128)(2,1)}, u32[]{:S(2)}, u32[]{:S(2)}) async-start(bf16[8,4,512,1024]{3,2,1,0:T(8,128)(2,1)} %bitcast.382), calls=%async_computation.2 | async-start | bytes 67108864 | tf_op jit(solution)/shard_map/all_to_all | solution.py:82
  161.2 16.0 copy-start.43
  165.1 8.0 copy-start.31
  165.1 8.0 copy-start.32
  165.1 8.7 copy-start.33
  165.1 8.7 copy-start.34
  169.1 5.3 copy-start.54
  169.4 11.5 copy-start.7
  172.0 5.1 copy-start.38
  693.0 370.1 %all-to-all-start.3 = ((bf16[8,4,512,1024]{3,2,1,0:T(8,128)(2,1)}), bf16[8,4,512,1024]{3,2,1,0:T(8,128)(2,1)}, u32[]{:S(2)}, u32[]{:S(2)}) async-start(bf16[8,4,512,1024]{3,2,1,0:T(8,128)(2,1)} %copy.119), calls=%async_computation.3 | async-start | bytes 67108864 | tf_op jit(solution)/shard_map/all_to_all | solution.py:96
  699.2 5.3 copy-start.53
  699.3 5.9 copy-start.41
  699.3 6.8 copy-start.40
  699.3 7.6 copy-start.30
  699.3 8.7 copy-start.29
  699.3 9.7 copy-start.35
  699.3 10.1 copy-start.48
  700.6 16.3 copy-start.44
  700.6 16.3 copy-start.51
  730.9 24.5 %copy-start.13 = (bf16[1024,1024]{0,1:T(8,128)(2,1)S(1)}, bf16[1024,1024]{0,1:T(8,128)(2,1)}, u32[]{:S(2)}) copy-start(bf16[1024,1024]{0,1:T(8,128)(2,1)} %copy.98) | copy-start | bytes 6291460
  755.4 6.5 copy-start.8
  755.4 6.5 copy-start.17
  755.4 6.5 copy-start.18
  785.6 21.6 copy-start.25
  807.3 59.3 %copy-start.23 = (f32[8,2,1024]{2,1,0:T(2,128)}, f32[8,2,1024]{2,1,0:T(2,128)S(1)}, u32[]{:S(2)}) copy-start(f32[8,2,1024]{2,1,0:T(2,128)S(1)} %fusion.12) | copy-start | bytes 196612
  859.7 6.9 copy-start.42
  859.7 203.5 %copy-start.2 = (s32[8192]{0:T(1024)S(1)}, s32[8192]{0:T(1024)}, u32[]{:S(2)}) copy-start(s32[8192]{0:T(1024)} %reshape.183) | copy-start | bytes 98308
  1063.1 161.7 %copy-start.28 = (pred[1024,8]{1,0:T(8,128)(4,1)S(1)}, pred[1024,8]{1,0:T(8,128)(4,1)}, u32[]{:S(2)}) copy-start(pred[1024,8]{1,0:T(8,128)(4,1)} %copy.111) | copy-start | bytes 24580
  1398.7 370.1 %all-to-all-start = ((bf16[8,4,512,1024]{3,2,1,0:T(8,128)(2,1)}), bf16[8,4,512,1024]{3,2,1,0:T(8,128)(2,1)}, u32[]{:S(2)}, u32[]{:S(2)}) async-start(bf16[8,4,512,1024]{3,2,1,0:T(8,128)(2,1)} %bitcast.383), calls=%async_computation | async-start | bytes 67108864 | tf_op jit(solution)/shard_map/all_to_all | solution.py:71
  1862.6 369.9 %all-to-all-start.1 = ((bf16[8,4,512,1024]{3,2,1,0:T(8,128)(2,1)}), bf16[8,4,512,1024]{3,2,1,0:T(8,128)(2,1)}, u32[]{:S(2)}, u32[]{:S(2)}) async-start(bf16[8,4,512,1024]{3,2,1,0:T(8,128)(2,1)} %copy.108), calls=%async_computation.1 | async-start | bytes 67108864 | tf_op jit(solution)/shard_map/all_to_all | solution.py:76
  1868.7 4.8 copy-start.49
  1868.7 5.4 copy-start.9
  1868.7 5.4 copy-start.19
  1868.7 5.4 copy-start.26
  1868.7 5.4 copy-start.36
  1873.4 40.6 %copy-start.21 = (bf16[1024,16,64]{0,2,1:T(8,128)(2,1)}, bf16[1024,16,64]{0,2,1:T(8,128)(2,1)S(1)}, u32[]{:S(2)}) copy-start(bf16[1024,16,64]{0,2,1:T(8,128)(2,1)S(1)} %fusion.107) | copy-start | bytes 6291460
  1874.1 39.9 %copy-start.15 = (pred[1024,1024]{1,0:T(8,128)(4,1)S(1)}, pred[1024,1024]{1,0:T(8,128)(4,1)}, u32[]{:S(2)}) copy-start(pred[1024,1024]{1,0:T(8,128)(4,1)} %iota_compare_fusion) | copy-start | bytes 3145732
  1874.1 39.9 %copy-start.24 = (f32[8,2,1024]{2,1,0:T(2,128)S(1)}, f32[8,2,1024]{2,1,0:T(2,128)}, u32[]{:S(2)}) copy-start(f32[8,2,1024]{2,1,0:T(2,128)} %copy-done.23) | copy-start | bytes 196612
  1999.3 17.6 copy-start.45
  1999.3 17.6 copy-start.47
  2016.9 6.2 copy-start.39
  2016.9 6.2 copy-start.4
  2016.9 6.2 copy-start.10
  2046.1 186.5 %copy-start.1 = (s32[8192]{0:T(1024)S(1)}, s32[8192]{0:T(1024)}, u32[]{:S(2)}) copy-start(s32[8192]{0:T(1024)} %reshape.177) | copy-start | bytes 98308
  2232.6 161.6 %copy-start.22 = (f32[1024,8]{1,0:T(8,128)S(1)}, f32[1024,8]{1,0:T(8,128)}, u32[]{:S(2)}) copy-start(f32[1024,8]{1,0:T(8,128)} %copy.193) | copy-start | bytes 98308
  2232.6 161.6 %copy-start.27 = (pred[1024,8]{1,0:T(8,128)(4,1)S(1)}, pred[1024,8]{1,0:T(8,128)(4,1)}, u32[]{:S(2)}) copy-start(pred[1024,8]{1,0:T(8,128)(4,1)} %copy.103) | copy-start | bytes 24580
  (14 other events, 52.7 us)
where the time goes:
time: 2440 us; the launch traced here: 2430 us
  waiting for transfers between devices  923 us (38%)
  local copies, waits for them, and re-layouts  702 us (29%)
  matrix products  583 us (24%)
  other arithmetic  193 us (8%)
  starting transfers between devices  24.6 us (1%)
    gather x2, local copies, waits for them, and re-layouts, pick_rows(): return buf.at[expert_ids, safe_slots].get(mode='fill', fill_value=0)  323 us
    unnamed x133, local copies, waits for them, and re-layouts  307 us
    all_to_all x1, waiting for transfers between devices, local_step(): d_out = lax.all_to_all(send_b, 'expert', 0, 0, tiled=True)  286 us
    all_to_all x1, waiting for transfers between devices, local_step(): recv_a = lax.all_to_all(send_a, 'expert', 0, 0, tiled=True)  259 us
    all_to_all x1, waiting for transfers between devices, local_step(): lax.all_to_all(grad_in, 'expert', 0, 0, tiled=True)  196 us
    all_to_all x1, waiting for transfers between devices, local_step(): lax.all_to_all(out_a, 'expert', 0, 0, tiled=True)  182 us
    dot_general x4, matrix products, attn_out(): jnp.einsum('grtm,mge->tgre', probs, val_proj, preferred_element_type=jnp....  100 us
    dot_general x3, matrix products, attn_out(): jnp.einsum('tgre,mge->grtm', query, key_proj, preferred_element_type=jnp....  55.4 us
  transfers between devices with their start and end apart: 4, of which 4 were waited for; matrix products, arithmetic and copies ran while one was open for 22% of the time, Pallas kernels for 0%

commit v1 on v0

v1 whole, which is shorter than its diff:
```python
import functools

import jax
import jax.numpy as jnp
from jax import lax
from jax.experimental import pallas as pl
from jax.experimental.pallas import tpu as pltpu
from jax.sharding import PartitionSpec as P

NORM_EPS = 1e-6


def expert_map(expert_ids, slot_ids, gates, experts):
    held = (expert_ids[None] == jnp.arange(experts)[:, None, None]) & (slot_ids >= 0)[None]
    slot_map = jnp.max(jnp.where(held, slot_ids[None], -1), axis=2).astype(jnp.float32)
    gate_map = jnp.sum(jnp.where(held, gates.astype(jnp.float32)[None], 0.0), axis=2)
    return slot_map, gate_map


VMEM_BYTES = 60 * 2 ** 20
NT = (((1,), (1,)), ((), ()))
TN = (((0,), (0,)), ((), ()))


def mm(lhs, rhs, dims=(((1,), (0,)), ((), ()))):
    return lax.dot_general(lhs, rhs, dims, preferred_element_type=jnp.float32)


def round_bf16(values):
    return values.astype(jnp.bfloat16).astype(jnp.float32)


def fill_sizes(capacity):
    return (capacity * 9 // 16 // 16 * 16, capacity)


def by_fill(count, capacity, body):
    low = 0
    for size in fill_sizes(capacity):
        pl.when((count > low) & (count <= size))(functools.partial(body, size))
        low = size


def forward_kernel(capacity, counts, slot_rows, slot_cols, gate_cols, x_ref, w1_ref, w3_ref, w2_ref, out_ref):
    source = pl.program_id(0)
    tokens = x_ref.shape[1]
    out_ref[...] = jnp.zeros_like(out_ref)
    for expert in range(w1_ref.shape[0]):
        def body(size, expert=expert):
            rows = lax.broadcasted_iota(jnp.int32, (size, tokens), 0)
            hot = jnp.where(slot_rows[0, expert:expert + 1, :] == rows, 1.0, 0.0).astype(jnp.bfloat16)
            buf = mm(hot, x_ref[0]).astype(jnp.bfloat16)
            act_1 = round_bf16(mm(buf, w1_ref[expert]))
            act_3 = round_bf16(mm(buf, w3_ref[expert]))
            hidden = (act_1 * jax.nn.sigmoid(act_1) * act_3).astype(jnp.bfloat16)
            out = mm(hidden, w2_ref[expert]).astype(jnp.bfloat16)
            cols = lax.broadcasted_iota(jnp.int32, (tokens, size), 1)
            mix = jnp.where(slot_cols[0, :, expert:expert + 1] == cols, gate_cols[0, :, expert:expert + 1], 0.0).astype(jnp.bfloat16)
            out_ref[0] += mm(mix, out)

        by_fill(counts[source, expert], capacity, body)


def experts_forward(counts, slot_rows, slot_cols, gate_cols, rows, w_1, w_3, w_2, capacity):
    group, tokens, model_dim = rows.shape
    local, _, ff = w_1.shape
    whole = lambda shape: pl.BlockSpec(shape, lambda p: (0, 0, 0), pipeline_mode=pl.Buffered(1))
    by_source = lambda shape: pl.BlockSpec(shape, lambda p: (p, 0, 0))
    return pl.pallas_call(
        functools.partial(forward_kernel, capacity),
        out_shape=jax.ShapeDtypeStruct((group, tokens, model_dim), jnp.float32),
        grid=(group,),
        in_specs=[pl.BlockSpec(memory_space=pltpu.SMEM), by_source((1, local, tokens)), by_source((1, tokens, local)), by_source((1, tokens, local)),
                  by_source((1, tokens, model_dim)), whole(w_1.shape), whole(w_3.shape), whole(w_2.shape)],
        out_specs=by_source((1, tokens, model_dim)),
        compiler_params=pltpu.CompilerParams(dimension_semantics=('arbitrary',), vmem_limit_bytes=VMEM_BYTES),
        cost_estimate=pl.CostEstimate(flops=group * local * capacity * model_dim * (4 * tokens + 6 * ff) // 2, bytes_accessed=group * tokens * model_dim * 6, transcendentals=0),
        name='experts_forward',
    )(counts, slot_rows, slot_cols, gate_cols, rows, w_1, w_3, w_2)


def backward_kernel(capacity, counts, slot_rows, gate_rows, dy_ref, u_ref, w1_ref, w3_ref, w2_ref, du_ref, g1_ref, g2_ref, g3_ref):
    expert, source = pl.program_id(0), pl.program_id(1)
    tokens = dy_ref.shape[1]

    @pl.when(source == 0)
    def _():
        g1_ref[...] = jnp.zeros_like(g1_ref)
        g2_ref[...] = jnp.zeros_like(g2_ref)
        g3_ref[...] = jnp.zeros_like(g3_ref)

    def body(size):
        rows = lax.broadcasted_iota(jnp.int32, (size, tokens), 0)
        scaled = jnp.where(slot_rows[0, 0] == rows, gate_rows[0, 0], 0.0).astype(jnp.bfloat16)
        d_out = mm(scaled, dy_ref[0]).astype(jnp.bfloat16)
        saved = u_ref[0, :size, :]
        pre_1 = round_bf16(mm(saved, w1_ref[0]))
        pre_3 = round_bf16(mm(saved, w3_ref[0]))
        sigma = jax.nn.sigmoid(pre_1)
        silu_1 = pre_1 * sigma
        hidden = (silu_1 * pre_3).astype(jnp.bfloat16)
        g2_ref[0] += mm(hidden, d_out, TN)
        grad_hid = round_bf16(mm(d_out, w2_ref[0], NT))
        grad_a1 = (grad_hid * pre_3 * sigma * (1.0 + pre_1 * (1.0 - sigma))).astype(jnp.bfloat16)
        grad_a3 = (grad_hid * silu_1).astype(jnp.bfloat16)
        g1_ref[0] += mm(saved, grad_a1, TN)
        g3_ref[0] += mm(saved, grad_a3, TN)
        du_ref[0, :size, :] = (mm(grad_a1, w1_ref[0], NT) + mm(grad_a3, w3_ref[0], NT)).astype(jnp.bfloat16)

    by_fill(counts[source, expert], capacity, body)


def experts_backward(counts, slot_rows, gate_rows, dy_rows, saved, w_1, w_3, w_2, capacity):
    group, tokens, model_dim = dy_rows.shape
    local, _, ff = w_1.shape
    by_pair = lambda shape: pl.BlockSpec(shape, lambda e, p: (p, e, 0, 0))
    by_expert = lambda shape: pl.BlockSpec(shape, lambda e, p: (e, 0, 0))
    by_slot = pl.BlockSpec((1, capacity, model_dim), lambda e, p: (e, p, 0))
    return pl.pallas_call(
        functools.partial(backward_kernel, capacity),
        out_shape=(jax.ShapeDtypeStruct(saved.shape, jnp.bfloat16),) + tuple(jax.ShapeDtypeStruct(w.shape, jnp.float32) for w in (w_1, w_2, w_3)),
        grid=(local, group),
        in_specs=[pl.BlockSpec(memory_space=pltpu.SMEM), by_pair((1, 1, 1, tokens)), by_pair((1, 1, 1, tokens)), pl.BlockSpec((1, tokens, model_dim), lambda e, p: (p, 0, 0)),
                  by_slot, by_expert((1, model_dim, ff)), by_expert((1, model_dim, ff)), by_expert((1, ff, model_dim))],
        out_specs=(by_slot, by_expert((1, model_dim, ff)), by_expert((1, ff, model_dim)), by_expert((1, model_dim, ff))),
        compiler_params=pltpu.CompilerParams(dimension_semantics=('arbitrary', 'arbitrary'), vmem_limit_bytes=VMEM_BYTES),
        cost_estimate=pl.CostEstimate(flops=group * local * capacity * model_dim * (2 * tokens + 16 * ff) // 2, bytes_accessed=saved.size * 4, transcendentals=0),
        name='experts_backward',
    )(counts, slot_rows[:, :, None, :], gate_rows[:, :, None, :], dy_rows, saved, w_1, w_3, w_2)


def combine_kernel(capacity, counts, slot_cols, buf_ref, out_ref):
    source = pl.program_id(0)
    tokens = out_ref.shape[1]
    out_ref[...] = jnp.zeros_like(out_ref)
    for expert in range(buf_ref.shape[0]):
        def body(size, expert=expert):
            cols = lax.broadcasted_iota(jnp.int32, (tokens, size), 1)
            mix = jnp.where(slot_cols[0, :, expert:expert + 1] == cols, 1.0, 0.0).astype(jnp.bfloat16)
            out_ref[0] += mm(mix, buf_ref[expert, :size, :])

        by_fill(counts[source, expert], capacity, body)


def combine_rows(counts, slot_cols, buf, capacity):
    group, tokens, local = slot_cols.shape
    model_dim = buf.shape[-1]
    return pl.pallas_call(
        functools.partial(combine_kernel, capacity),
        out_shape=jax.ShapeDtypeStruct((group, tokens, model_dim), jnp.float32),
        grid=(group,),
        in_specs=[pl.BlockSpec(memory_space=pltpu.SMEM), pl.BlockSpec((1, tokens, local), lambda p: (p, 0, 0)), pl.BlockSpec((local, capacity, model_dim), lambda p: (0, p, 0))],
        out_specs=pl.BlockSpec((1, tokens, model_dim), lambda p: (p, 0, 0)),
        compiler_params=pltpu.CompilerParams(dimension_semantics=('arbitrary',), vmem_limit_bytes=VMEM_BYTES),
        cost_estimate=pl.CostEstimate(flops=group * local * capacity * model_dim * tokens, bytes_accessed=group * tokens * model_dim * 8, transcendentals=0),
        name='combine_rows',
    )(counts, slot_cols, buf)


def lane_iota(shape):
    return lax.broadcasted_iota(jnp.int32, shape, len(shape) - 1)


def norm_rows(values, gain):
    scale = lax.rsqrt(jnp.mean(values * values, axis=-1, keepdims=True) + NORM_EPS)
    return values * scale, scale, (values * scale * gain).astype(jnp.bfloat16)


def norm_pull(values, gain, cotangent):
    scaled, scale, _ = norm_rows(values, gain)
    inner = cotangent * gain
    grad = scale * (inner - scaled * jnp.mean(inner * scaled, axis=-1, keepdims=True))
    return grad, jnp.sum(cotangent * scaled, axis=0, keepdims=True)


def project_kernel(score_scale, x_ref, gain_ref, w_ref, q_ref, k_ref, v_ref):
    normed = norm_rows(x_ref[...].astype(jnp.float32), gain_ref[...].astype(jnp.float32))[2]
    groups = q_ref.shape[0]
    width = q_ref.shape[2]
    mixed = round_bf16(mm(normed, w_ref[...]))
    for group in range(groups):
        q_ref[group] = (mixed[:, group * width:(group + 1) * width] * score_scale).astype(jnp.bfloat16)
    low = lane_iota((x_ref.shape[0], width)) < width // 2
    for start, ref in ((groups, k_ref), (groups * 3 // 2, v_ref)):
        for pair in range(groups // 2):
            both = mixed[:, (start + pair) * width:(start + pair + 1) * width]
            turned = pltpu.roll(both, width // 2, 1)
            ref[2 * pair] = jnp.where(low, both, turned).astype(jnp.bfloat16)
            ref[2 * pair + 1] = jnp.where(low, turned, both).astype(jnp.bfloat16)


def twin(rows, size):
    both = jnp.concatenate([rows, rows], axis=0)
    own = (lax.broadcasted_iota(jnp.int32, both.shape, 0) < size) == (lane_iota(both.shape) < both.shape[1] // 2)
    return jnp.where(own, both, jnp.zeros_like(both))


def untwin(columns, size):
    low = lax.broadcasted_iota(jnp.int32, (columns.shape[0], size), 0) < columns.shape[0] // 2
    return jnp.where(low, columns[:, :size], columns[:, size:]).T


def pieces(index, size):
    return ([(0, index * size)] if index else []) + [(index * size, (index + 1) * size)]


def causal_scores(k_ref, queries, start, stop, index, size):
    scores = mm(k_ref[0, start:stop, :], queries, NT)
    if start == index * size:
        column = lane_iota(scores.shape)
        row = lax.broadcasted_iota(jnp.int32, scores.shape, 0)
        scores = jnp.where(row <= jnp.where(column >= size, column - size, column), scores, -1e30)
    return scores


def attend_kernel(size, q_ref, k_ref, v_ref, out_ref, stat_ref):
    tokens = q_ref.shape[1]
    values_t = v_ref[0].T
    for index in range(tokens // size):
        rows = pl.ds(index * size, size)
        queries = twin(q_ref[0, rows, :], size)
        spans = pieces(index, size)
        scores = [causal_scores(k_ref, queries, a, b, index, size) for a, b in spans]
        top = functools.reduce(jnp.maximum, [jnp.max(part, axis=0, keepdims=True) for part in scores])
        exps = [jnp.exp(part - top) for part in scores]
        inverse = 1.0 / sum(jnp.sum(part, axis=0, keepdims=True) for part in exps)
        out = sum(mm(values_t[:, a:b], (part * inverse).astype(jnp.bfloat16)) for (a, b), part in zip(spans, exps))
        out_ref[0, rows, :] = untwin(out, size).astype(jnp.bfloat16)
        stat_ref[0, index, 0:1, :] = top
        stat_ref[0, index, 1:2, :] = inverse


def attend_pull_kernel(size, score_scale, q_ref, k_ref, v_ref, d_ref, stat_ref, dq_ref, dk_ref, dv_ref, dk_sum, dv_sum):
    tokens = q_ref.shape[1]
    width = q_ref.shape[2]
    keys_t = k_ref[0].T
    dk_sum[...] = jnp.zeros_like(dk_sum)
    dv_sum[...] = jnp.zeros_like(dv_sum)
    for index in range(tokens // size):
        rows = pl.ds(index * size, size)
        queries = twin(q_ref[0, rows, :], size)
        cotangent = twin(d_ref[0, rows, :], size)
        top = stat_ref[0, index, 0:1, :]
        inverse = stat_ref[0, index, 1:2, :]
        spans = pieces(index, size)
        probs, grads = [], []
        for a, b in spans:
            part = jnp.exp(causal_scores(k_ref, queries, a, b, index, size) - top) * inverse
            probs.append(part)
            dv_sum[a:b, :] += mm(part.astype(jnp.bfloat16), cotangent)
            grads.append(round_bf16(mm(v_ref[0, a:b, :], cotangent, NT)))
        inner = sum(jnp.sum(p * g, axis=0, keepdims=True) for p, g in zip(probs, grads))
        out = 0.0
        for (a, b), p, g in zip(spans, probs, grads):
            pull = (p * (g - inner)).astype(jnp.bfloat16)
            dk_sum[a:b, :] += mm(pull, queries)
            out = out + mm(keys_t[:, a:b], pull)
        dq_ref[0, rows, :] = (untwin(out, size) * score_scale).astype(jnp.bfloat16)
    dk_ref[0] = (dk_sum[...] + pltpu.roll(dk_sum[...], width // 2, 1)).astype(jnp.bfloat16)
    dv_ref[0] = (dv_sum[...] + pltpu.roll(dv_sum[...], width // 2, 1)).astype(jnp.bfloat16)


def merge_kernel(x_ref, gain_ref, ctx_ref, w_ref, h_ref, u_ref):
    context = jnp.concatenate([ctx_ref[group] for group in range(ctx_ref.shape[0])], axis=1)
    attn = round_bf16(mm(context, w_ref[...]))
    h_rows = (x_ref[...].astype(jnp.float32) + attn).astype(jnp.bfloat16)
    h_ref[...] = h_rows
    u_ref[...] = norm_rows(h_rows.astype(jnp.float32), gain_ref[...].astype(jnp.float32))[2]


def call(kernel, name, out_shape, flops, grid=(), **specs):
    return pl.pallas_call(
        kernel, out_shape=out_shape, grid=grid, name=name,
        compiler_params=pltpu.CompilerParams(dimension_semantics=('arbitrary',) * len(grid), vmem_limit_bytes=VMEM_BYTES),
        cost_estimate=pl.CostEstimate(flops=flops, bytes_accessed=2 ** 24, transcendentals=0), **specs)


def attention_forward(x, gain_1, gain_2, w_qkv, w_out, groups):
    tokens, model_dim = x.shape
    width = model_dim // groups
    block = tokens // 4
    heads = jax.ShapeDtypeStruct((groups, tokens, width), jnp.bfloat16)
    like = jax.ShapeDtypeStruct(x.shape, jnp.bfloat16)
    rows = pl.BlockSpec((block, model_dim), lambda i: (i, 0))
    head_rows = pl.BlockSpec((groups, block, width), lambda i: (0, i, 0))
    fixed = lambda array: pl.BlockSpec(array.shape, lambda i: (0, 0))
    query, key, value = call(functools.partial(project_kernel, (width // 2) ** -0.5), 'project', (heads,) * 3, 4 * tokens * model_dim ** 2, (4,),
                             in_specs=[rows, fixed(gain_1), fixed(w_qkv)], out_specs=(head_rows,) * 3)(x, gain_1, w_qkv)
    head = pl.BlockSpec((1, tokens, width), lambda g: (g, 0, 0))
    stat_shape = (groups, 4, 2, 2 * block)
    stat = pl.BlockSpec((1,) + stat_shape[1:], lambda g: (g, 0, 0, 0))
    context, stats = call(functools.partial(attend_kernel, block), 'attend', (heads, jax.ShapeDtypeStruct(stat_shape, jnp.float32)), 16 * tokens ** 2 * model_dim, (groups,),
                          in_specs=[head] * 3, out_specs=(head, stat))(query, key, value)
    h_rows, u_rows = call(merge_kernel, 'merge', (like, like), 2 * tokens * model_dim ** 2, (4,),
                          in_specs=[rows, fixed(gain_2), head_rows, fixed(w_out)], out_specs=(rows, rows))(x, gain_2, context, w_out)
    return h_rows, u_rows, (query, key, value, context, stats)


def out_pull_kernel(h_ref, dy_ref, du_ref, gain_ref, ctx_ref, w_ref, dh_ref, dctx_ref, grad_o_ref, grad_n_ref):
    groups, tokens, width = ctx_ref.shape
    gain = gain_ref[...].astype(jnp.float32)
    block = tokens // 4
    total = 0.0
    for index in range(4):
        rows = pl.ds(index * block, block)
        grad, part = norm_pull(h_ref[rows, :].astype(jnp.float32), gain, round_bf16(du_ref[rows, :]))
        total = total + part
        d_rows = (dy_ref[rows, :].astype(jnp.float32) + round_bf16(grad)).astype(jnp.bfloat16)
        dh_ref[rows, :] = d_rows
        pulled = mm(d_rows, w_ref[...], NT).astype(jnp.bfloat16)
        for group in range(groups):
            dctx_ref[group, rows, :] = pulled[:, group * width:(group + 1) * width]
    grad_n_ref[...] = round_bf16(total)
    for group in range(0, groups, 2):
        context = jnp.concatenate([ctx_ref[group], ctx_ref[group + 1]], axis=1)
        grad_o_ref[group * width:(group + 2) * width, :] = round_bf16(mm(context, dh_ref[...], TN))


def in_pull_kernel(x_ref, dh_ref, dq_ref, dk_ref, dv_ref, gain_ref, w_ref, dx_ref, gq_ref, gk_ref, gv_ref, gn_ref, normed_ref, mixed_ref):
    groups, tokens, width = dq_ref.shape
    model_dim = x_ref.shape[1]
    gain = gain_ref[...].astype(jnp.float32)
    block = tokens // 4
    low = lane_iota((block, width)) < width // 2
    total = 0.0
    for index in range(4):
        rows = pl.ds(index * block, block)
        for group in range(groups):
            mixed_ref[rows, group * width:(group + 1) * width] = dq_ref[group, rows, :]
        for start, ref in ((groups, dk_ref), (groups * 3 // 2, dv_ref)):
            for pair in range(groups // 2):
                mixed_ref[rows, (start + pair) * width:(start + pair + 1) * width] = jnp.where(low, ref[2 * pair, rows, :], ref[2 * pair + 1, rows, :])
        values = x_ref[rows, :].astype(jnp.float32)
        normed_ref[rows, :] = norm_rows(values, gain)[2]
        grad, part = norm_pull(values, gain, round_bf16(mm(mixed_ref[rows, :], w_ref[...], NT)))
        total = total + part
        dx_ref[rows, :] = (dh_ref[rows, :].astype(jnp.float32) + round_bf16(grad)).astype(jnp.bfloat16)
    gn_ref[...] = round_bf16(total)
    half = model_dim // 2
    for start, ref in ((0, gq_ref), (2, gk_ref), (3, gv_ref)):
        for part in range(ref.shape[1] // half):
            ref[:, part * half:(part + 1) * half] = round_bf16(mm(normed_ref[...], mixed_ref[:, (start + part) * half:(start + part + 1) * half], TN))


def attention_backward(x, dy, du, h_rows, saved, gain_1, gain_2, w_qkv, w_out):
    query, key, value, context, stats = saved
    groups, tokens, width = query.shape
    model_dim = x.shape[1]
    heads = jax.ShapeDtypeStruct(query.shape, jnp.bfloat16)
    like = jax.ShapeDtypeStruct(x.shape, jnp.bfloat16)
    wide = lambda *shape: jax.ShapeDtypeStruct(shape, jnp.float32)
    dh, d_context, grad_o, grad_n2 = call(out_pull_kernel, 'out_pull', (like, heads, wide(model_dim, model_dim), wide(1, model_dim)), 4 * tokens * model_dim ** 2)(
        h_rows, dy, du, gain_2, context, w_out)
    head = pl.BlockSpec((1, tokens, width), lambda g: (g, 0, 0))
    stat = pl.BlockSpec((1,) + stats.shape[1:], lambda g: (g, 0, 0, 0))
    d_query, d_key, d_value = call(functools.partial(attend_pull_kernel, tokens // 4, (width // 2) ** -0.5), 'attend_pull', (heads,) * 3, 40 * tokens ** 2 * model_dim, (groups,),
                                   in_specs=[head] * 4 + [stat], out_specs=(head,) * 3, scratch_shapes=[pltpu.VMEM((tokens, width), jnp.float32)] * 2)(query, key, value, d_context, stats)
    dx, grad_q, grad_k, grad_v, grad_n1 = call(
        in_pull_kernel, 'in_pull', (like, wide(model_dim, model_dim), wide(model_dim, model_dim // 2), wide(model_dim, model_dim // 2), wide(1, model_dim)), 8 * tokens * model_dim ** 2,
        scratch_shapes=[pltpu.VMEM((tokens, model_dim), jnp.bfloat16), pltpu.VMEM((tokens, 2 * model_dim), jnp.bfloat16)])(x, dh, d_query, d_key, d_value, gain_1, w_qkv)
    return dx, grad_q, grad_k, grad_v, grad_o, grad_n1, grad_n2


def solution(mesh):
    group = mesh.shape['expert']

    def local_step(x_a, x_b, dy_b, eid_a, slot_a, gate_a, eid_b, slot_b, gate_b, u_b, norm_1, norm_2, w_q, w_k, w_v, w_o, w_1, w_2, w_3):
        local_experts = w_1.shape[0]
        experts = local_experts * group
        capacity = u_b.shape[1] // group
        model_dim = x_a.shape[1]

        tokens = x_a.shape[0]
        meta = jnp.stack([*expert_map(eid_a, slot_a, gate_a, experts), *expert_map(eid_b, slot_b, gate_b, experts)], axis=1)
        meta = lax.all_to_all(meta.reshape(group, local_experts, 4, tokens), 'expert', 0, 0, tiled=True)
        slots_a, gates_a, slots_b, gates_b = (meta[:, :, i] for i in range(4))
        rows_a, rows_b = slots_a.astype(jnp.int32), slots_b.astype(jnp.int32)
        counts_a, counts_b = (jnp.sum((rows >= 0).astype(jnp.int32), axis=2) for rows in (rows_a, rows_b))
        cols_a, cols_b = jnp.swapaxes(rows_a, 1, 2), jnp.swapaxes(rows_b, 1, 2)

        all_dy = lax.all_gather(dy_b, 'expert', axis=0, tiled=True).reshape(group, tokens, model_dim)
        kv_heads = w_k.shape[1]
        w_qkv = jnp.concatenate([w_q.reshape(model_dim, -1), w_k.reshape(model_dim, -1), w_v.reshape(model_dim, -1)], axis=1)
        w_out = w_o.reshape(-1, model_dim)
        gain_1, gain_2 = norm_1[None], norm_2[None]
        h_a, u_a, _ = attention_forward(x_a, gain_1, gain_2, w_qkv, w_out, kv_heads)
        all_u = lax.all_gather(u_a, 'expert', axis=0, tiled=True).reshape(group, tokens, model_dim)
        h_b, _, kept_b = attention_forward(x_b, gain_1, gain_2, w_qkv, w_out, kv_heads)

        grad_in, grad_w1, grad_w2, grad_w3 = experts_backward(counts_b, rows_b, gates_b, all_dy, u_b, w_1, w_3, w_2, capacity)
        part_b = combine_rows(counts_b, cols_b, grad_in, capacity)
        du_rows = lax.psum_scatter(part_b.reshape(group * tokens, model_dim), 'expert', scatter_dimension=0, tiled=True)

        part_a = experts_forward(counts_a, rows_a, cols_a, jnp.swapaxes(gates_a, 1, 2), all_u, w_1, w_3, w_2, capacity)
        mixed = lax.psum_scatter(part_a.reshape(group * tokens, model_dim), 'expert', scatter_dimension=0, tiled=True)
        y_a = (h_a.astype(jnp.float32) + mixed).astype(jnp.bfloat16)
        dx_b, g_q, g_k, g_v, g_o, g_n1, g_n2 = attention_backward(x_b, dy_b, du_rows, h_b, kept_b, gain_1, gain_2, w_qkv, w_out)
        return (y_a, dx_b, grad_w1, grad_w2, grad_w3, g_q.reshape((1,) + w_q.shape), g_k.reshape((1,) + w_k.shape), g_v.reshape((1,) + w_v.shape), g_o.reshape((1,) + w_o.shape), g_n1, g_n2)

    row_spec = P(('data', 'expert'), None)
    cube_spec = P(('data', 'expert'), None, None)
    quad_spec = P(('data', 'expert'), None, None, None)
    expert_spec = P('expert', None, None)
    in_specs = (row_spec, row_spec, row_spec, row_spec, row_spec, row_spec, row_spec, row_spec, row_spec, cube_spec, P(), P(), P(), P(), P(), P(), expert_spec, expert_spec, expert_spec)
    out_specs = (row_spec, row_spec, cube_spec, cube_spec, cube_spec, quad_spec, quad_spec, quad_spec, quad_spec, row_spec, row_spec)
    return jax.shard_map(local_step, mesh=mesh, in_specs=in_specs, out_specs=out_specs, check_vma=False)
```

time: 2440 us -> 721 us (0.30)
  waiting for transfers between devices: 923 us -> 162 us
  local copies, waits for them, and re-layouts: 702 us -> 34.6 us
  matrix products: 583 us -> 0 us
  Pallas kernels: 0 us -> 453 us
  other arithmetic: 193 us -> 30.2 us
  starting transfers between devices: 24.6 us -> 0.16 us
    all_to_all x4 -> x0, waiting for transfers between devices: 923 us -> none  [the longest x1 286 us: local_step(): d_out = lax.all_to_all(send_b, 'expert', 0, 0, tiled=True)]
    dot_general x24 -> x0, matrix products: 522 us -> none  [the longest x4 100 us: attn_out(): jnp.einsum('grtm,mge->tgre', probs, val_proj, preferred_element_type=jnp....]
    pallas_call x0 -> x12, Pallas kernels: none -> 453 us  [the longest x1 151 us: experts_backward(): pl.pallas_call(functools.partial(backward_kernel, capacity), out_shape=(j...]
    gather x2 -> x0, local copies, waits for them, and re-layouts: 323 us -> none  [pick_rows(): return buf.at[expert_ids, safe_slots].get(mode='fill', fill_value=0)]
    unnamed x133 -> x21, local copies, waits for them, and re-layouts: 307 us -> 8.07 us
    reduce_scatter x0 -> x2, waiting for transfers between devices: none -> 158 us  [the longest x1 120 us: local_step(): lax.psum_scatter(part_a.reshape(group * tokens, model_dim), 'expert', sca...]
    mul x2 -> x0, other arithmetic: 53.3 us -> none  [the longest x1 44.3 us: attn_out(): jnp.einsum('tgre,mge->grtm', query, key_proj, preferred_element_type=jnp....]
    convert_element_type x3 -> x4, local copies, waits for them, and re-layouts: 49.4 us -> 7.02 us  [the longest x2 6.95 us: local_step(): rows_a, rows_b = (slots_a.astype(jnp.int32), slots_b.astype(jnp.int32))]
  transfers between devices with their start and end apart: 4 -> 4, of which waited for: 4 -> 3; matrix products, arithmetic and copies ran while one was open for 22% -> 8% of each run, Pallas kernels for 0% -> 63%
where the time goes in v1:
time: 721 us; the launch traced here: 715 us
  Pallas kernels  453 us (63%)
  waiting for transfers between devices  162 us (22%)
  local copies, waits for them, and re-layouts  34.6 us (5%)
  other arithmetic  30.2 us (4%)
  blocking collectives  20.3 us (3%)
  between operations  14.3 us (2%)
    pallas_call x1, Pallas kernels, experts_backward(): pl.pallas_call(functools.partial(backward_kernel, capacity), out_shape=(j...  151 us
    reduce_scatter x1, waiting for transfers between devices, local_step(): lax.psum_scatter(part_a.reshape(group * tokens, model_dim), 'expert', sca...  120 us
    pallas_call x1, Pallas kernels, experts_forward(): pl.pallas_call(functools.partial(forward_kernel, capacity), out_shape=jax...  104 us
    pallas_call x1, Pallas kernels, combine_rows(): pl.pallas_call(functools.partial(combine_kernel, capacity), out_shape=jax...  49 us
    pallas_call x2, Pallas kernels, attention_forward(): call(functools.partial(attend_kernel, block), 'attend', (heads, jax.Shape...  46.6 us
    pallas_call x1, Pallas kernels, attention_backward(): call(functools.partial(attend_pull_kernel, tokens // 4, (width // 2) ** (...  38.5 us
    reduce_scatter x1, waiting for transfers between devices, local_step(): lax.psum_scatter(part_b.reshape(group * tokens, model_dim), 'expert', sca...  38 us
    all_to_all x1, blocking collectives, local_step(): lax.all_to_all(meta.reshape(group, local_experts, 4, tokens), 'expert', 0...  20.3 us
  transfers between devices with their start and end apart: 4, of which 3 were waited for; matrix products, arithmetic and copies ran while one was open for 8% of the time, Pallas kernels for 63%

profile of v1, /device:TPU:0, one launch (start us, length us, event | category | flops | bytes accessed | tf_op | source)
XLA Modules:
  0.0 714.8 jit_solution(2755610231476309806)
XLA Ops:
  7.2 0.0 all-gather.5.cloned.1.call-start
  7.2 0.7 all-gather.5.cloned.1.call-update
  7.9 0.0 all-gather.3.cloned.1.call-start
  8.0 2.9 copy.92
  10.9 1.5 copy.93
  12.4 2.3 copy.94
  14.6 0.6 broadcast_in_dim.54.gain_ref
  15.2 0.6 broadcast_in_dim.53.gain_ref
  15.8 3.3 pad_maximum_fusion.w_ref
  19.1 9.5 %project.2 = (bf16[8,1024,128]{2,1,0:T(8,128)(2,1)}, bf16[8,1024,128]{2,1,0:T(8,128)(2,1)}, bf16[8,1024,128]{2,1,0:T(8,128)(2,1)}) custom-call(bf16[1024,1024]{1,0:T(8,128)(2,1)} %x_ref.6, bf16[1,1024]{1,0:T(2,128)(2,1)} %broadcast_in_dim.54.gain_ref, bf16[1024,2048]{1,0:T(8,128)(2,1)} %pad_maximum_fusion.w_ref), custom_call_target="tpu_custom_call" | custom-call | flops 4294967296 | bytes 16777216 | tf_op jit(solution)/shard_map/project/pallas_call | solution.py:287
  28.6 23.3 %attend.2 = (bf16[8,1024,128]{2,1,0:T(8,128)(2,1)}, f32[8,4,2,512]{3,2,1,0:T(2,128)}) custom-call(bf16[8,1024,128]{2,1,0:T(8,128)(2,1)} %get-tuple-element.39.q_ref, bf16[8,1024,128]{2,1,0:T(8,128)(2,1)} %get-tuple-element.40.k_ref, bf16[8,1024,128]{2,1,0:T(8,128)(2,1)} %get-tuple-element.41.v_ref), custom_call_target="tpu_custom_call" | custom-call | flops 17179869184 | bytes 16777216 | tf_op jit(solution)/shard_map/attend/pallas_call | solution.py:292
  52.0 7.2 %merge.2 = (bf16[1024,1024]{1,0:T(8,128)(2,1)}, bf16[1024,1024]{1,0:T(8,128)(2,1)}) custom-call(bf16[1024,1024]{1,0:T(8,128)(2,1)} %x_ref.6, bf16[1,1024]{1,0:T(2,128)(2,1)} %broadcast_in_dim.53.gain_ref, bf16[8,1024,128]{2,1,0:T(8,128)(2,1)} %get-tuple-element.42.ctx_ref, bf16[1024,1024]{1,0:T(8,128)(2,1)} %bitcast.40), custom_call_target="tpu_custom_call" | custom-call | flops 2147483648 | bytes 16777216 | tf_op jit(solution)/shard_map/merge/pallas_call | solution.py:294
  59.2 0.0 reduce-scatter.5.cloned.1.call-start
  59.2 0.6 select_reduce_fusion.3
  59.9 0.6 select_reduce_fusion.1
  60.6 0.4 select_reduce_fusion.2
  61.1 0.4 select_reduce_fusion
  61.5 0.1 pad_maximum_fusion.1
  61.7 0.3 copy.95
  62.0 20.3 %all_to_all.5 = f32[8,4,4,1024]{3,2,1,0:T(4,128)S(1)} all-to-all(f32[8,4,4,1024]{3,2,1,0:T(4,128)S(1)} %copy.95), channel_id=1, replica_groups=mesh['data'=1,'expert'=8] {'expert'}, dimensions={0} | all-to-all | bytes 1048576 | tf_op jit(solution)/shard_map/all_to_all | solution.py:375
  82.3 1.1 fusion.3
  83.4 2.7 copy.106
  86.0 6.3 fusion.2
  92.4 3.5 copy.100.slot_rows
  95.8 3.6 convert_reduce_fusion.counts
  99.4 2.9 all-gather.5.cloned.1.call-done
  102.4 150.8 %experts_backward.1 = (bf16[4,4096,1024]{2,1,0:T(8,128)(2,1)}, f32[4,1024,512]{2,1,0:T(8,128)}, f32[4,512,1024]{2,1,0:T(8,128)}, f32[4,1024,512]{2,1,0:T(8,128)}) custom-call(s32[8,4]{1,0:T(8,128)} %convert_reduce_fusion.counts, s32[8,4,1,1024]{3,2,1,0:T(1,128)} %copy.100.slot_rows, f32[8,4,1,1024]{3,2,1,0:T(1,128)} %get-tuple-element.82.gate_rows, ...), custom_call_target="tpu_custom_call" | custom-call | flops 85899345920 | bytes 67108864 | tf_op jit(solution)/shard_map/experts_backward/pallas_call | solution.py:119
  253.2 49.0 %combine_rows.1 = f32[8,1024,1024]{2,1,0:T(8,128)} custom-call(s32[8,4]{1,0:T(8,128)} %convert_reduce_fusion.counts, s32[8,1024,4]{2,1,0:T(8,128)} %get-tuple-element.79.slot_cols, bf16[4,4096,1024]{2,1,0:T(8,128)(2,1)} %get-tuple-element.50.buf_ref), custom_call_target="tpu_custom_call" | custom-call | flops 17179869184 | bytes 67108864 | tf_op jit(solution)/shard_map/combine_rows/pallas_call | solution.py:148
  302.2 0.0 reduce-scatter.3.cloned.1.call-start
  302.2 2.7 copy.104
  304.9 6.3 convert_bitcast_fusion
  311.2 3.5 copy.98.slot_rows
  314.7 2.7 copy.105
  317.4 3.6 convert_reduce_fusion.1.counts
  321.0 104.5 %experts_forward.1 = f32[8,1024,1024]{2,1,0:T(8,128)} custom-call(s32[8,4]{1,0:T(8,128)} %convert_reduce_fusion.1.counts, s32[8,4,1024]{2,1,0:T(4,128)} %copy.98.slot_rows, s32[8,1024,4]{2,1,0:T(8,128)} %get-tuple-element.80.slot_cols, f32[8,1024,4]{2,1,0:T(8,128)} %bitcast.32, bf16[8,1024,1024]{2,1,0:T(8,128)(2,1)} %bitcast.39, ...), custom_call_target="tpu_custom_call" | custom-call | flops 60129542144 | bytes 50331648 | tf_op jit(solution)/shard_map/experts_forward/pallas_call | solution.py:69
  425.4 0.0 reduce-scatter.3.cloned.1.call-update
  425.5 9.5 %project.3 = (bf16[8,1024,128]{2,1,0:T(8,128)(2,1)}, bf16[8,1024,128]{2,1,0:T(8,128)(2,1)}, bf16[8,1024,128]{2,1,0:T(8,128)(2,1)}) custom-call(bf16[1024,1024]{1,0:T(8,128)(2,1)} %x_ref.9, bf16[1,1024]{1,0:T(2,128)(2,1)} %broadcast_in_dim.54.gain_ref, bf16[1024,2048]{1,0:T(8,128)(2,1)} %pad_maximum_fusion.w_ref), custom_call_target="tpu_custom_call" | custom-call | flops 4294967296 | bytes 16777216 | tf_op jit(solution)/shard_map/project/pallas_call | solution.py:287
  435.0 23.3 %attend.3 = (bf16[8,1024,128]{2,1,0:T(8,128)(2,1)}, f32[8,4,2,512]{3,2,1,0:T(2,128)}) custom-call(bf16[8,1024,128]{2,1,0:T(8,128)(2,1)} %get-tuple-element.45.q_ref, bf16[8,1024,128]{2,1,0:T(8,128)(2,1)} %get-tuple-element.46.k_ref, bf16[8,1024,128]{2,1,0:T(8,128)(2,1)} %get-tuple-element.47.v_ref), custom_call_target="tpu_custom_call" | custom-call | flops 17179869184 | bytes 16777216 | tf_op jit(solution)/shard_map/attend/pallas_call | solution.py:292
  458.3 7.1 merge.3
  465.4 38.0 %reduce-scatter.5.cloned.1.call-done.du_ref = f32[1024,1024]{1,0:T(8,128)} async-done(((f32[8192,1024]{1,0:T(8,128)}), f32[1024,1024]{1,0:T(8,128)}) %reduce-scatter.5.cloned.1.call-update) | async-done | bytes 4194320 | tf_op jit(solution)/shard_map/reduce_scatter | solution.py:392
  503.5 13.0 %out_pull.1 = (bf16[1024,1024]{1,0:T(8,128)(2,1)}, bf16[8,1024,128]{2,1,0:T(8,128)(2,1)}, f32[1024,1024]{1,0:T(8,128)}, f32[1,1024]{1,0:T(1,128)}) custom-call(bf16[1024,1024]{1,0:T(8,128)(2,1)} %get-tuple-element.49.h_ref, bf16[1024,1024]{1,0:T(8,128)(2,1)} %dy_ref.1, f32[1024,1024]{1,0:T(8,128)} %reduce-scatter.5.cloned.1.call-done.du_ref, ...), custom_call_target="tpu_custom_call" | custom-call | flops 4294967296 | bytes 16777216 | tf_op jit(solution)/shard_map/out_pull/pallas_call | solution.py:352
  516.4 38.5 %attend_pull.1 = (bf16[8,1024,128]{2,1,0:T(8,128)(2,1)}, bf16[8,1024,128]{2,1,0:T(8,128)(2,1)}, bf16[8,1024,128]{2,1,0:T(8,128)(2,1)}) custom-call(bf16[8,1024,128]{2,1,0:T(8,128)(2,1)} %get-tuple-element.45.q_ref, bf16[8,1024,128]{2,1,0:T(8,128)(2,1)} %get-tuple-element.46.k_ref, bf16[8,1024,128]{2,1,0:T(8,128)(2,1)} %get-tuple-element.47.v_ref, ...), custom_call_target="tpu_custom_call" | custom-call | flops 42949672960 | bytes 16777216 | tf_op jit(solution)/shard_map/attend_pull/pallas_call | solution.py:356
  554.9 17.7 %in_pull.1 = (bf16[1024,1024]{1,0:T(8,128)(2,1)}, f32[1024,1024]{1,0:T(8,128)}, f32[1024,512]{1,0:T(8,128)}, f32[1024,512]{1,0:T(8,128)}, f32[1,1024]{1,0:T(1,128)}) custom-call(bf16[1024,1024]{1,0:T(8,128)(2,1)} %x_ref.9, bf16[1024,1024]{1,0:T(8,128)(2,1)} %get-tuple-element.51.dh_ref, bf16[8,1024,128]{2,1,0:T(8,128)(2,1)} %get-tuple-element.54.dq_ref, ...), custom_call_target="tpu_custom_call" | custom-call | flops 8589934592 | bytes 16777216 | tf_op jit(solution)/shard_map/in_pull/pallas_call | solution.py:358
  572.6 5.3 copy.101
  577.9 3.0 copy.102
  580.9 1.8 copy.103
  582.8 120.3 %reduce-scatter.3.cloned.1.call-done = f32[1024,1024]{1,0:T(8,128)} async-done(((f32[8192,1024]{1,0:T(8,128)}), f32[1024,1024]{1,0:T(8,128)}) %reduce-scatter.3.cloned.1.call-update) | async-done | bytes 4194320 | tf_op jit(solution)/shard_map/reduce_scatter | solution.py:395
  703.1 5.0 add_convert_fusion
  (31 shorter events, 0.3 us)
Async XLA Ops:
  7.2 95.2 %all-gather.5.cloned.1.call-start = ((), (), s32[]{:S(2)}) async-start(), calls=%async_computation.5 | async-start | bytes 18874368 | tf_op jit(solution)/shard_map/all_gather | solution.py:381
  7.9 313.1 %all-gather.3.cloned.1.call-start = ((), (), s32[]{:S(2)}) async-start(), calls=%async_computation.3 | async-start | bytes 18874368 | tf_op jit(solution)/shard_map/all_gather | solution.py:387
  8.0 6.7 copy-start.7
  8.0 7.3 %copy-start.8 = (bf16[1024]{0:T(1024)(128)(2,1)S(1)}, bf16[1024]{0:T(1024)(128)(2,1)}, u32[]{:S(2)}) copy-start(bf16[1024]{0:T(1024)(128)(2,1)} %param.30) | copy-start | bytes 6148
  51.9 7.3 %copy-start.1 = (s32[1024,8]{0,1:T(8,128)S(1)}, s32[1024,8]{0,1:T(8,128)}, u32[]{:S(2)}) copy-start(s32[1024,8]{0,1:T(8,128)} %param.23) | copy-start | bytes 98308
  51.9 7.3 %copy-start.3 = (s32[1024,8]{0,1:T(8,128)S(1)}, s32[1024,8]{0,1:T(8,128)}, u32[]{:S(2)}) copy-start(s32[1024,8]{0,1:T(8,128)} %param.22) | copy-start | bytes 98308
  51.9 7.9 %copy-start.2 = (s32[1024,8]{0,1:T(8,128)S(1)}, s32[1024,8]{0,1:T(8,128)}, u32[]{:S(2)}) copy-start(s32[1024,8]{0,1:T(8,128)} %param.26) | copy-start | bytes 98308
  51.9 8.0 %copy-start.4 = (s32[1024,8]{0,1:T(8,128)S(1)}, s32[1024,8]{0,1:T(8,128)}, u32[]{:S(2)}) copy-start(s32[1024,8]{0,1:T(8,128)} %param.25) | copy-start | bytes 98308
  52.0 8.6 %copy-start.5 = (bf16[1024,8]{0,1:T(8,128)(2,1)S(1)}, bf16[1024,8]{0,1:T(8,128)(2,1)}, u32[]{:S(2)}) copy-start(bf16[1024,8]{0,1:T(8,128)(2,1)} %param.24) | copy-start | bytes 49156
  52.0 9.1 %copy-start.6 = (bf16[1024,8]{0,1:T(8,128)(2,1)S(1)}, bf16[1024,8]{0,1:T(8,128)(2,1)}, u32[]{:S(2)}) copy-start(bf16[1024,8]{0,1:T(8,128)(2,1)} %param.27) | copy-start | bytes 49156
  59.2 444.3 %reduce-scatter.5.cloned.1.call-start = ((), (), s32[]{:S(2)}) async-start(), calls=%async_computation.6 | async-start | bytes 37748736 | tf_op jit(solution)/shard_map/reduce_scatter | solution.py:392
  302.2 400.9 %reduce-scatter.3.cloned.1.call-start = ((), (), s32[]{:S(2)}) async-start(), calls=%async_computation.4 | async-start | bytes 37748736 | tf_op jit(solution)/shard_map/reduce_scatter | solution.py:395
  577.9 3.0 copy-start
Sparse Core Ops, SparseCore 0:
  9.8 92.5 all-gather.4
  104.8 84.0 all-gather.2
  302.3 201.1 reduce-scatter.4
  506.8 196.2 reduce-scatter.2

commit v2 on v1

v2 whole, which is shorter than its diff:
```python
import functools

import jax
import jax.numpy as jnp
from jax import lax
from jax.experimental import pallas as pl
from jax.experimental.pallas import tpu as pltpu
from jax.sharding import PartitionSpec as P

NORM_EPS = 1e-6


def expert_map(expert_ids, slot_ids, gates, chosen):
    held = (expert_ids[None] == chosen[:, None, None]) & (slot_ids >= 0)[None]
    slot_map = jnp.max(jnp.where(held, slot_ids[None], -1), axis=2).astype(jnp.float32)
    gate_map = jnp.sum(jnp.where(held, gates.astype(jnp.float32)[None], 0.0), axis=2)
    return slot_map, gate_map


def swap(values, mask, group):
    return lax.ppermute(values, 'expert', [(i, i ^ mask) for i in range(group)])


VMEM_BYTES = 60 * 2 ** 20
NT = (((1,), (1,)), ((), ()))
TN = (((0,), (0,)), ((), ()))


def mm(lhs, rhs, dims=(((1,), (0,)), ((), ()))):
    return lax.dot_general(lhs, rhs, dims, preferred_element_type=jnp.float32)


def round_bf16(values):
    return values.astype(jnp.bfloat16).astype(jnp.float32)


def fill_sizes(capacity):
    return (capacity * 17 // 32 // 16 * 16, capacity)


def by_fill(count, capacity, body):
    low = 0
    for size in fill_sizes(capacity):
        pl.when((count > low) & (count <= size))(functools.partial(body, size))
        low = size


def pair_maps(meta_ref, first):
    rows = meta_ref[0, 0]
    cols = jnp.concatenate([rows, rows], axis=0).T
    return rows[first:first + 1].astype(jnp.int32), rows[first + 1:first + 2], cols[:, first:first + 1].astype(jnp.int32), cols[:, first + 1:first + 2]


def select_rows(slot, values, size):
    rows = lax.broadcasted_iota(jnp.int32, (size, slot.shape[1]), 0)
    return jnp.where(slot == rows, values, 0.0).astype(jnp.bfloat16)


def select_cols(slot, values, size):
    cols = lax.broadcasted_iota(jnp.int32, (slot.shape[0], size), 1)
    return jnp.where(slot == cols, values, 0.0).astype(jnp.bfloat16)


def forward_kernel(capacity, bit, counts, order, meta_ref, x_ref, w1_ref, w3_ref, w2_ref, *refs):
    out_ref = refs[-1]
    place, expert = pl.program_id(0), pl.program_id(1)

    @pl.when(expert == 0)
    def _():
        out_ref[...] = refs[0][...] if len(refs) > 1 else jnp.zeros_like(out_ref)

    def body(size):
        slot_row, _, slot_col, gate_col = pair_maps(meta_ref, 0)
        buf = mm(select_rows(slot_row, 1.0, size), x_ref[0]).astype(jnp.bfloat16)
        act_1 = round_bf16(mm(buf, w1_ref[expert]))
        act_3 = round_bf16(mm(buf, w3_ref[expert]))
        hidden = (act_1 * jax.nn.sigmoid(act_1) * act_3).astype(jnp.bfloat16)
        out = mm(hidden, w2_ref[expert]).astype(jnp.bfloat16)
        out_ref[0] += mm(select_cols(slot_col, gate_col, size), out)

    by_fill(counts[order[1, 2 * place + bit], expert], capacity, body)


def backward_kernel(capacity, bit, counts, order, meta_ref, dy_ref, u_ref, w1_ref, w3_ref, w2_ref, out_ref, d_ref, hid_ref, a1_ref, a3_ref):
    place, expert = pl.program_id(0), pl.program_id(1)

    @pl.when(expert == 0)
    def _():
        out_ref[...] = jnp.zeros_like(out_ref)

    def body(size):
        slot_row, gate_row, slot_col, _ = pair_maps(meta_ref, 2)
        d_out = mm(select_rows(slot_row, gate_row, size), dy_ref[0]).astype(jnp.bfloat16)
        d_ref[0, :size, :] = d_out
        saved = u_ref[0, :size, :]
        pre_1 = round_bf16(mm(saved, w1_ref[expert]))
        pre_3 = round_bf16(mm(saved, w3_ref[expert]))
        sigma = jax.nn.sigmoid(pre_1)
        silu_1 = pre_1 * sigma
        hid_ref[0, :size, :] = (silu_1 * pre_3).astype(jnp.bfloat16)
        grad_hid = round_bf16(mm(d_out, w2_ref[expert], NT))
        grad_a1 = (grad_hid * pre_3 * sigma * (1.0 + pre_1 * (1.0 - sigma))).astype(jnp.bfloat16)
        grad_a3 = (grad_hid * silu_1).astype(jnp.bfloat16)
        a1_ref[0, :size, :] = grad_a1
        a3_ref[0, :size, :] = grad_a3
        grad_in = (mm(grad_a1, w1_ref[expert], NT) + mm(grad_a3, w3_ref[expert], NT)).astype(jnp.bfloat16)
        out_ref[0] += mm(select_cols(slot_col, 1.0, size), grad_in)

    by_fill(counts[order[1, 2 * place + bit], expert], capacity, body)


def weights_kernel(capacity, counts, order, *refs):
    expert, place = pl.program_id(0), pl.program_id(1)
    g1_ref, g2_ref, g3_ref = refs[10:]

    @pl.when(place == 0)
    def _():
        g1_ref[...] = jnp.zeros_like(g1_ref)
        g2_ref[...] = jnp.zeros_like(g2_ref)
        g3_ref[...] = jnp.zeros_like(g3_ref)

    for bit in range(2):
        u_ref, d_ref, hid_ref, a1_ref, a3_ref = refs[5 * bit:5 * bit + 5]

        def body(size):
            g2_ref[0] += mm(hid_ref[0, :size, :], d_ref[0, :size, :], TN)
            g1_ref[0] += mm(u_ref[0, :size, :], a1_ref[0, :size, :], TN)
            g3_ref[0] += mm(u_ref[0, :size, :], a3_ref[0, :size, :], TN)

        by_fill(counts[order[1, 2 * place + bit], expert], capacity, body)


def ordered_call(kernel, name, out_shape, flops, grid, in_specs, out_specs):
    return pl.pallas_call(
        kernel, out_shape=out_shape, name=name,
        grid_spec=pltpu.PrefetchScalarGridSpec(num_scalar_prefetch=2, grid=grid, in_specs=in_specs, out_specs=out_specs),
        compiler_params=pltpu.CompilerParams(dimension_semantics=('arbitrary',) * len(grid), vmem_limit_bytes=VMEM_BYTES),
        cost_estimate=pl.CostEstimate(flops=flops, bytes_accessed=2 ** 24, transcendentals=0))


def pair_specs(bit, meta, rows, weights):
    pair = pl.BlockSpec((1, 1) + meta.shape[2:], lambda i, e, counts, order: (order[1, 2 * i + bit], e, 0, 0))
    source = pl.BlockSpec((1,) + rows.shape[1:], lambda i, e, counts, order: (order[0, 2 * i + bit], 0, 0))
    whole = [pl.BlockSpec(w.shape, lambda i, e, counts, order: (0, 0, 0), pipeline_mode=pl.Buffered(1)) for w in weights]
    part = pl.BlockSpec((1,) + rows.shape[1:], lambda i, e, counts, order: (i, 0, 0))
    return pair, source, whole, part


def experts_forward(bit, counts, order, meta, rows, weights, capacity, *start):
    group, tokens, model_dim = rows.shape
    local, _, ff = weights[0].shape
    pair, source, whole, part = pair_specs(bit, meta, rows, weights)
    return ordered_call(functools.partial(forward_kernel, capacity, bit), 'experts_forward', jax.ShapeDtypeStruct((group // 2, tokens, model_dim), jnp.float32),
                        group * local * capacity * model_dim * (4 * tokens + 6 * ff) // 4, (group // 2, local), [pair, source] + whole + [part] * len(start), part)(counts, order, meta, rows, *weights, *start)


def experts_backward(bit, counts, order, meta, rows, saved, weights, capacity):
    group, tokens, model_dim = rows.shape
    local, _, ff = weights[0].shape
    pair, source, whole, part = pair_specs(bit, meta, rows, weights)
    stored = pl.BlockSpec((1, capacity, model_dim), lambda i, e, counts, order: (e, order[0, 2 * i + bit], 0))
    slots = lambda width: pl.BlockSpec((1, capacity, width), lambda i, e, counts, order: (e, i, 0))
    kept = lambda width: jax.ShapeDtypeStruct((local, group // 2 * capacity, width), jnp.bfloat16)
    return ordered_call(functools.partial(backward_kernel, capacity, bit), 'experts_backward',
                        (jax.ShapeDtypeStruct((group // 2, tokens, model_dim), jnp.float32), kept(model_dim), kept(ff), kept(ff), kept(ff)),
                        group * local * capacity * model_dim * (4 * tokens + 10 * ff) // 4, (group // 2, local),
                        [pair, source, stored] + whole, (part, slots(model_dim), slots(ff), slots(ff), slots(ff)))(counts, order, meta, rows, saved, *weights)


def experts_weights(counts, order, saved, kept_near, kept_far, capacity):
    local, slots_all, model_dim = saved.shape
    ff = kept_near[1].shape[2]
    slots = lambda width: pl.BlockSpec((1, capacity, width), lambda e, i, counts, order: (e, i, 0))
    stored = lambda bit: pl.BlockSpec((1, capacity, model_dim), lambda e, i, counts, order: (e, order[0, 2 * i + bit], 0))
    shapes = ((model_dim, ff), (ff, model_dim), (model_dim, ff))
    inner = [slots(model_dim), slots(ff), slots(ff), slots(ff)]
    return ordered_call(functools.partial(weights_kernel, capacity), 'experts_weights', tuple(jax.ShapeDtypeStruct((local,) + shape, jnp.float32) for shape in shapes),
                        local * slots_all * model_dim * 6 * ff // 2, (local, slots_all // capacity // 2),
                        [stored(0)] + inner + [stored(1)] + inner,
                        tuple(pl.BlockSpec((1,) + shape, lambda e, i, counts, order: (e, 0, 0)) for shape in shapes))(counts, order, saved, *kept_near, saved, *kept_far)


def lane_iota(shape):
    return lax.broadcasted_iota(jnp.int32, shape, len(shape) - 1)


def norm_rows(values, gain):
    scale = lax.rsqrt(jnp.mean(values * values, axis=-1, keepdims=True) + NORM_EPS)
    return values * scale, scale, (values * scale * gain).astype(jnp.bfloat16)


def norm_pull(values, gain, cotangent):
    scaled, scale, _ = norm_rows(values, gain)
    inner = cotangent * gain
    grad = scale * (inner - scaled * jnp.mean(inner * scaled, axis=-1, keepdims=True))
    return grad, jnp.sum(cotangent * scaled, axis=0, keepdims=True)


def project_kernel(score_scale, x_ref, gain_ref, w_ref, q_ref, k_ref, v_ref):
    normed = norm_rows(x_ref[...].astype(jnp.float32), gain_ref[...].astype(jnp.float32))[2]
    groups = q_ref.shape[0]
    width = q_ref.shape[2]
    mixed = round_bf16(mm(normed, w_ref[...], NT))
    for group in range(groups):
        q_ref[group] = (mixed[:, group * width:(group + 1) * width] * score_scale).astype(jnp.bfloat16)
    low = lane_iota((x_ref.shape[0], width)) < width // 2
    for start, ref in ((groups, k_ref), (groups * 3 // 2, v_ref)):
        for pair in range(groups // 2):
            both = mixed[:, (start + pair) * width:(start + pair + 1) * width]
            turned = pltpu.roll(both, width // 2, 1)
            ref[2 * pair] = jnp.where(low, both, turned).astype(jnp.bfloat16)
            ref[2 * pair + 1] = jnp.where(low, turned, both).astype(jnp.bfloat16)


def twin(rows, size):
    both = jnp.concatenate([rows, rows], axis=0)
    own = (lax.broadcasted_iota(jnp.int32, both.shape, 0) < size) == (lane_iota(both.shape) < both.shape[1] // 2)
    return jnp.where(own, both, jnp.zeros_like(both))


def untwin(columns, size):
    low = lax.broadcasted_iota(jnp.int32, (columns.shape[0], size), 0) < columns.shape[0] // 2
    return jnp.where(low, columns[:, :size], columns[:, size:]).T


def pieces(index, size):
    return ([(0, index * size)] if index else []) + [(index * size, (index + 1) * size)]


def causal_scores(k_ref, queries, start, stop, index, size):
    scores = mm(k_ref[0, start:stop, :], queries, NT)
    if start == index * size:
        column = lane_iota(scores.shape)
        row = lax.broadcasted_iota(jnp.int32, scores.shape, 0)
        scores = jnp.where(row <= jnp.where(column >= size, column - size, column), scores, -1e30)
    return scores


def attend_kernel(size, q_ref, k_ref, v_ref, out_ref, stat_ref):
    tokens = q_ref.shape[1]
    values_t = v_ref[0].T
    for index in range(tokens // size):
        rows = pl.ds(index * size, size)
        queries = twin(q_ref[0, rows, :], size)
        spans = pieces(index, size)
        scores = [causal_scores(k_ref, queries, a, b, index, size) for a, b in spans]
        top = functools.reduce(jnp.maximum, [jnp.max(part, axis=0, keepdims=True) for part in scores])
        exps = [jnp.exp(part - top) for part in scores]
        inverse = 1.0 / sum(jnp.sum(part, axis=0, keepdims=True) for part in exps)
        out = sum(mm(values_t[:, a:b], (part * inverse).astype(jnp.bfloat16)) for (a, b), part in zip(spans, exps))
        out_ref[0, rows, :] = untwin(out, size).astype(jnp.bfloat16)
        stat_ref[0, index, 0:1, :] = top
        stat_ref[0, index, 1:2, :] = inverse


def attend_pull_kernel(size, score_scale, q_ref, k_ref, v_ref, d_ref, stat_ref, dq_ref, dk_ref, dv_ref, dk_sum, dv_sum):
    tokens = q_ref.shape[1]
    width = q_ref.shape[2]
    keys_t = k_ref[0].T
    dk_sum[...] = jnp.zeros_like(dk_sum)
    dv_sum[...] = jnp.zeros_like(dv_sum)
    for index in range(tokens // size):
        rows = pl.ds(index * size, size)
        queries = twin(q_ref[0, rows, :], size)
        cotangent = twin(d_ref[0, rows, :], size)
        top = stat_ref[0, index, 0:1, :]
        inverse = stat_ref[0, index, 1:2, :]
        spans = pieces(index, size)
        probs, grads = [], []
        for a, b in spans:
            part = jnp.exp(causal_scores(k_ref, queries, a, b, index, size) - top) * inverse
            probs.append(part)
            dv_sum[a:b, :] += mm(part.astype(jnp.bfloat16), cotangent)
            grads.append(round_bf16(mm(v_ref[0, a:b, :], cotangent, NT)))
        inner = sum(jnp.sum(p * g, axis=0, keepdims=True) for p, g in zip(probs, grads))
        out = 0.0
        for (a, b), p, g in zip(spans, probs, grads):
            pull = (p * (g - inner)).astype(jnp.bfloat16)
            dk_sum[a:b, :] += mm(pull, queries)
            out = out + mm(keys_t[:, a:b], pull)
        dq_ref[0, rows, :] = (untwin(out, size) * score_scale).astype(jnp.bfloat16)
    dk_ref[0] = (dk_sum[...] + pltpu.roll(dk_sum[...], width // 2, 1)).astype(jnp.bfloat16)
    dv_ref[0] = (dv_sum[...] + pltpu.roll(dv_sum[...], width // 2, 1)).astype(jnp.bfloat16)


def merge_kernel(x_ref, gain_ref, ctx_ref, w_ref, h_ref, u_ref):
    context = jnp.concatenate([ctx_ref[group] for group in range(ctx_ref.shape[0])], axis=1)
    attn = round_bf16(mm(context, w_ref[...]))
    h_rows = (x_ref[...].astype(jnp.float32) + attn).astype(jnp.bfloat16)
    h_ref[...] = h_rows
    u_ref[...] = norm_rows(h_rows.astype(jnp.float32), gain_ref[...].astype(jnp.float32))[2]


def call(kernel, name, out_shape, flops, grid=(), **specs):
    return pl.pallas_call(
        kernel, out_shape=out_shape, grid=grid, name=name,
        compiler_params=pltpu.CompilerParams(dimension_semantics=('arbitrary',) * len(grid), vmem_limit_bytes=VMEM_BYTES),
        cost_estimate=pl.CostEstimate(flops=flops, bytes_accessed=2 ** 24, transcendentals=0), **specs)


def project(x, gain_1, w_qkv, groups):
    tokens, model_dim = x.shape
    width = model_dim // groups
    block = tokens // 4
    rows = pl.BlockSpec((block, model_dim), lambda i: (i, 0))
    head_rows = pl.BlockSpec((groups, block, width), lambda i: (0, i, 0))
    fixed = lambda array: pl.BlockSpec(array.shape, lambda i: (0, 0))
    return call(functools.partial(project_kernel, (width // 2) ** -0.5), 'project', (jax.ShapeDtypeStruct((groups, tokens, width), jnp.bfloat16),) * 3, 4 * tokens * model_dim ** 2, (4,),
                in_specs=[rows, fixed(gain_1), fixed(w_qkv)], out_specs=(head_rows,) * 3)(x, gain_1, w_qkv)


def attention_forward(x, projected, gain_2, w_out):
    query, key, value = projected
    groups, tokens, width = query.shape
    model_dim = x.shape[1]
    block = tokens // 4
    heads = jax.ShapeDtypeStruct(query.shape, jnp.bfloat16)
    like = jax.ShapeDtypeStruct(x.shape, jnp.bfloat16)
    rows = pl.BlockSpec((block, model_dim), lambda i: (i, 0))
    head_rows = pl.BlockSpec((groups, block, width), lambda i: (0, i, 0))
    fixed = lambda array: pl.BlockSpec(array.shape, lambda i: (0, 0))
    head = pl.BlockSpec((1, tokens, width), lambda g: (g, 0, 0))
    stat_shape = (groups, 4, 2, 2 * block)
    stat = pl.BlockSpec((1,) + stat_shape[1:], lambda g: (g, 0, 0, 0))
    context, stats = call(functools.partial(attend_kernel, block), 'attend', (heads, jax.ShapeDtypeStruct(stat_shape, jnp.float32)), 16 * tokens ** 2 * model_dim, (groups,),
                          in_specs=[head] * 3, out_specs=(head, stat))(query, key, value)
    h_rows, u_rows = call(merge_kernel, 'merge', (like, like), 2 * tokens * model_dim ** 2, (4,),
                          in_specs=[rows, fixed(gain_2), head_rows, fixed(w_out)], out_specs=(rows, rows))(x, gain_2, context, w_out)
    return h_rows, u_rows, (query, key, value, context, stats)


def out_pull_kernel(h_ref, dy_ref, du_ref, gain_ref, ctx_ref, w_ref, dh_ref, dctx_ref, grad_o_ref, grad_n_ref):
    groups, tokens, width = ctx_ref.shape
    gain = gain_ref[...].astype(jnp.float32)
    block = tokens // 4
    total = 0.0
    for index in range(4):
        rows = pl.ds(index * block, block)
        grad, part = norm_pull(h_ref[rows, :].astype(jnp.float32), gain, round_bf16(du_ref[rows, :]))
        total = total + part
        d_rows = (dy_ref[rows, :].astype(jnp.float32) + round_bf16(grad)).astype(jnp.bfloat16)
        dh_ref[rows, :] = d_rows
        pulled = mm(d_rows, w_ref[...], NT).astype(jnp.bfloat16)
        for group in range(groups):
            dctx_ref[group, rows, :] = pulled[:, group * width:(group + 1) * width]
    grad_n_ref[...] = round_bf16(total)
    for group in range(0, groups, 2):
        context = jnp.concatenate([ctx_ref[group], ctx_ref[group + 1]], axis=1)
        grad_o_ref[group * width:(group + 2) * width, :] = round_bf16(mm(context, dh_ref[...], TN))


def in_pull_kernel(x_ref, dh_ref, dq_ref, dk_ref, dv_ref, gain_ref, w_ref, dx_ref, gq_ref, gk_ref, gv_ref, gn_ref, normed_ref, mixed_ref):
    groups, tokens, width = dq_ref.shape
    model_dim = x_ref.shape[1]
    gain = gain_ref[...].astype(jnp.float32)
    block = tokens // 4
    low = lane_iota((block, width)) < width // 2
    total = 0.0
    for index in range(4):
        rows = pl.ds(index * block, block)
        for group in range(groups):
            mixed_ref[rows, group * width:(group + 1) * width] = dq_ref[group, rows, :]
        for start, ref in ((groups, dk_ref), (groups * 3 // 2, dv_ref)):
            for pair in range(groups // 2):
                mixed_ref[rows, (start + pair) * width:(start + pair + 1) * width] = jnp.where(low, ref[2 * pair, rows, :], ref[2 * pair + 1, rows, :])
        values = x_ref[rows, :].astype(jnp.float32)
        normed_ref[rows, :] = norm_rows(values, gain)[2]
        grad, part = norm_pull(values, gain, round_bf16(mm(mixed_ref[rows, :], w_ref[...])))
        total = total + part
        dx_ref[rows, :] = (dh_ref[rows, :].astype(jnp.float32) + round_bf16(grad)).astype(jnp.bfloat16)
    gn_ref[...] = round_bf16(total)
    half = model_dim // 2
    for start, ref in ((0, gq_ref), (2, gk_ref), (3, gv_ref)):
        for part in range(ref.shape[0] // half):
            ref[part * half:(part + 1) * half, :] = round_bf16(mm(mixed_ref[:, (start + part) * half:(start + part + 1) * half], normed_ref[...], TN))


def attention_pull(dy, du, h_rows, saved, gain_2, w_out):
    query, key, value, context, stats = saved
    groups, tokens, width = query.shape
    model_dim = dy.shape[1]
    heads = jax.ShapeDtypeStruct(query.shape, jnp.bfloat16)
    like = jax.ShapeDtypeStruct(dy.shape, jnp.bfloat16)
    wide = lambda *shape: jax.ShapeDtypeStruct(shape, jnp.float32)
    dh, d_context, grad_o, grad_n2 = call(out_pull_kernel, 'out_pull', (like, heads, wide(model_dim, model_dim), wide(1, model_dim)), 4 * tokens * model_dim ** 2)(
        h_rows, dy, du, gain_2, context, w_out)
    head = pl.BlockSpec((1, tokens, width), lambda g: (g, 0, 0))
    stat = pl.BlockSpec((1,) + stats.shape[1:], lambda g: (g, 0, 0, 0))
    d_query, d_key, d_value = call(functools.partial(attend_pull_kernel, tokens // 4, (width // 2) ** -0.5), 'attend_pull', (heads,) * 3, 40 * tokens ** 2 * model_dim, (groups,),
                                   in_specs=[head] * 4 + [stat], out_specs=(head,) * 3, scratch_shapes=[pltpu.VMEM((tokens, width), jnp.float32)] * 2)(query, key, value, d_context, stats)
    return dh, grad_o, grad_n2, (d_query, d_key, d_value)


def projection_pull(x, dh, pulls, gain_1, w_qkv):
    tokens, model_dim = x.shape
    like = jax.ShapeDtypeStruct(x.shape, jnp.bfloat16)
    wide = lambda *shape: jax.ShapeDtypeStruct(shape, jnp.float32)
    return call(
        in_pull_kernel, 'in_pull', (like, wide(model_dim, model_dim), wide(model_dim // 2, model_dim), wide(model_dim // 2, model_dim), wide(1, model_dim)), 8 * tokens * model_dim ** 2,
        scratch_shapes=[pltpu.VMEM((tokens, model_dim), jnp.bfloat16), pltpu.VMEM((tokens, 2 * model_dim), jnp.bfloat16)])(x, dh, *pulls, gain_1, w_qkv)


def solution(mesh):
    group = mesh.shape['expert']

    def local_step(x_a, x_b, dy_b, eid_a, slot_a, gate_a, eid_b, slot_b, gate_b, u_b, norm_1, norm_2, w_q, w_k, w_v, w_o, w_1, w_2, w_3):
        local_experts = w_1.shape[0]
        experts = local_experts * group
        capacity = u_b.shape[1] // group
        model_dim = x_a.shape[1]

        tokens = x_a.shape[0]
        me = lax.axis_index('expert')
        turned = me ^ jnp.arange(group, dtype=jnp.int32)
        places = (me % 2) ^ jnp.arange(group, dtype=jnp.int32)
        order = jnp.stack([places, places ^ me])
        chosen = (turned[:, None] * local_experts + jnp.arange(local_experts, dtype=jnp.int32)[None, :]).reshape(-1)
        meta = jnp.stack([*expert_map(eid_a, slot_a, gate_a, chosen), *expert_map(eid_b, slot_b, gate_b, chosen)], axis=1)
        meta = meta.reshape(group, local_experts, 4, tokens)
        meta = jnp.stack([meta[0]] + [swap(meta[r], r, group) for r in range(1, group)])
        counts_a, counts_b = (jnp.sum((meta[:, :, i] >= 0).astype(jnp.int32), axis=2) for i in (0, 2))
        weights = (w_1, w_3, w_2)

        all_dy = lax.all_gather(dy_b, 'expert', axis=0, tiled=True).reshape(group, tokens, model_dim)
        kv_heads = w_k.shape[1]
        w_qkv = jnp.concatenate([w.reshape(model_dim, -1).T for w in (w_q, w_k, w_v)], axis=0)
        w_out = w_o.reshape(-1, model_dim)
        gain_1, gain_2 = norm_1[None], norm_2[None]
        h_a, u_a, _ = attention_forward(x_a, project(x_a, gain_1, w_qkv, kv_heads), gain_2, w_out)
        all_u = lax.all_gather(u_a, 'expert', axis=0, tiled=True).reshape(group, tokens, model_dim)
        all_dy, projected_b = lax.optimization_barrier((all_dy, project(x_b, gain_1, w_qkv, kv_heads)))
        same_core = [[i for i in range(group) if i % 2 == core] for core in range(2)]
        reduce_chips = lambda part: lax.psum_scatter(part.reshape(-1, model_dim), 'expert', scatter_dimension=0, tiled=True, axis_index_groups=same_core)
        far_b, *kept_far = experts_backward(1, counts_b, order, meta, all_dy, u_b, weights, capacity)
        far_b, all_dy = lax.optimization_barrier((far_b, all_dy))
        came_b = swap(far_b, 1, group)
        near_b, *kept_near = experts_backward(0, counts_b, order, meta, all_dy, u_b, weights, capacity)
        part_b, all_u, kept_near = lax.optimization_barrier((near_b + came_b, all_u, kept_near))
        du_rows = reduce_chips(part_b)
        far_a = experts_forward(1, counts_a, order, meta, all_u, weights, capacity)
        far_a, projected_b, all_u = lax.optimization_barrier((far_a, projected_b, all_u))
        came_a = swap(far_a, 1, group)
        h_b, _, kept_b = attention_forward(x_b, projected_b, gain_2, w_out)
        came_a, h_b = lax.optimization_barrier((came_a, h_b))
        part_a = experts_forward(0, counts_a, order, meta, all_u, weights, capacity, came_a)
        part_a, kept_near, du_rows = lax.optimization_barrier((part_a, kept_near, du_rows))
        mixed = reduce_chips(part_a)
        dh_b, g_o, g_n2, pulls_b = attention_pull(dy_b, du_rows, h_b, kept_b, gain_2, w_out)
        dx_b, g_q, g_k, g_v, g_n1 = projection_pull(x_b, dh_b, pulls_b, gain_1, w_qkv)
        dx_b, kept_near = lax.optimization_barrier((dx_b, kept_near))
        grad_w1, grad_w2, grad_w3 = experts_weights(counts_b, order, u_b, kept_near, kept_far, capacity)
        mixed, grad_w1 = lax.optimization_barrier((mixed, grad_w1))
        y_a = (h_a.astype(jnp.float32) + mixed).astype(jnp.bfloat16)
        return (y_a, dx_b, grad_w1, grad_w2, grad_w3, g_q.T.reshape((1,) + w_q.shape), g_k.T.reshape((1,) + w_k.shape), g_v.T.reshape((1,) + w_v.shape), g_o.reshape((1,) + w_o.shape), g_n1, g_n2)

    row_spec = P(('data', 'expert'), None)
    cube_spec = P(('data', 'expert'), None, None)
    quad_spec = P(('data', 'expert'), None, None, None)
    expert_spec = P('expert', None, None)
    in_specs = (row_spec, row_spec, row_spec, row_spec, row_spec, row_spec, row_spec, row_spec, row_spec, cube_spec, P(), P(), P(), P(), P(), P(), expert_spec, expert_spec, expert_spec)
    out_specs = (row_spec, row_spec, cube_spec, cube_spec, cube_spec, quad_spec, quad_spec, quad_spec, quad_spec, row_spec, row_spec)
    return jax.shard_map(local_step, mesh=mesh, in_specs=in_specs, out_specs=out_specs, check_vma=False)
```

time: 721 us -> 580 us (0.80)
  waiting for transfers between devices: 162 us -> 39.1 us
  local copies, waits for them, and re-layouts: 34.6 us -> 3.17 us
  Pallas kernels: 453 us -> 477 us
  blocking collectives: 20.3 us -> 0 us
  starting transfers between devices: 0.16 us -> 9.38 us
    reduce_scatter x2, waiting for transfers between devices: 158 us -> 14.6 us  [local_step(): lax.psum_scatter(part.reshape(-1, model_dim), 'expert', scatter_dimension...]
    pallas_call x8 -> x10, Pallas kernels: 392 us -> 416 us  [the longest x2 140 us: experts_backward(): ordered_call(functools.partial(backward_kernel, capacity, bit), 'experts_...]
    all_to_all x1 -> x0, blocking collectives: 20.3 us -> none  [local_step(): lax.all_to_all(meta.reshape(group, local_experts, 4, tokens), 'expert', 0...]
    add x0 -> x2, other arithmetic: none -> 17.1 us  [the longest x1 17 us: local_step(): near_b + came_b]
    all_gather x1, waiting for transfers between devices: 2.93 us -> 14.4 us  [local_step(): lax.all_gather(dy_b, 'expert', axis=0, tiled=True)]
    pallas_call x3 -> x0, local copies, waits for them, and re-layouts: 10.2 us -> none  [attention_backward(): call(in_pull_kernel, 'in_pull', (like, wide(model_dim, model_dim), wide(m...]
    ppermute x0 -> x9, waiting for transfers between devices: none -> 9.41 us  [swap(): return lax.ppermute(values, 'expert', [(i, i ^ mask) for i in range(group)])]
    ppermute x0 -> x9, starting transfers between devices: none -> 9.23 us  [swap(): return lax.ppermute(values, 'expert', [(i, i ^ mask) for i in range(group)])]
  transfers between devices with their start and end apart: 4 -> 13, of which waited for: 3 -> 5; matrix products, arithmetic and copies ran while one was open for 8% -> 5% of each run, Pallas kernels for 63% -> 83%
where the time goes in v2:
time: 580 us; the launch traced here: 573 us
  Pallas kernels  477 us (82%)
  waiting for transfers between devices  39.1 us (7%)
  other arithmetic  30.1 us (5%)
  between operations  14.2 us (2%)
  starting transfers between devices  9.38 us (2%)
    pallas_call x2, Pallas kernels, experts_backward(): ordered_call(functools.partial(backward_kernel, capacity, bit), 'experts_...  140 us
    pallas_call x2, Pallas kernels, experts_forward(): ordered_call(functools.partial(forward_kernel, capacity, bit), 'experts_f...  116 us
    pallas_call x1, Pallas kernels, experts_weights(): ordered_call(functools.partial(weights_kernel, capacity), 'experts_weight...  71.9 us
    pallas_call x2, Pallas kernels, attention_forward(): call(functools.partial(attend_kernel, block), 'attend', (heads, jax.Shape...  46.6 us
    pallas_call x1, Pallas kernels, attention_pull(): call(functools.partial(attend_pull_kernel, tokens // 4, (width // 2) ** (...  38.7 us
    pallas_call x2, Pallas kernels, project(): call(functools.partial(project_kernel, (width // 2) ** (-0.5)), 'project'...  19.2 us
    pallas_call x1, Pallas kernels, projection_pull(): call(in_pull_kernel, 'in_pull', (like, wide(model_dim, model_dim), wide(m...  17.7 us
    add x1, other arithmetic, local_step(): near_b + came_b  17 us
  transfers between devices with their start and end apart: 13, of which 5 were waited for; matrix products, arithmetic and copies ran while one was open for 5% of the time, Pallas kernels for 83%

profile of v2, /device:TPU:0, one launch (start us, length us, event | category | flops | bytes accessed | tf_op | source)
XLA Modules:
  0.0 573.1 jit_solution(4178342562884731444)
XLA Ops:
  7.2 0.7 all-gather.3.cloned.1.call-update
  7.9 0.0 all-gather.5.cloned.1.call-start
  8.0 1.3 broadcast_in_dim.53.gain_ref
  9.2 1.3 broadcast_in_dim.52.gain_ref
  10.5 3.7 pad_maximum_fusion.w_ref
  14.2 9.4 %project.2 = (bf16[8,1024,128]{2,1,0:T(8,128)(2,1)}, bf16[8,1024,128]{2,1,0:T(8,128)(2,1)}, bf16[8,1024,128]{2,1,0:T(8,128)(2,1)}) custom-call(bf16[1024,1024]{1,0:T(8,128)(2,1)} %x_ref.6, bf16[1,1024]{1,0:T(2,128)(2,1)} %broadcast_in_dim.53.gain_ref, bf16[2048,1024]{1,0:T(8,128)(2,1)} %pad_maximum_fusion.w_ref), custom_call_target="tpu_custom_call" | custom-call | flops 4294967296 | bytes 16777216 | tf_op jit(solution)/shard_map/project/pallas_call | solution.py:308
  23.6 23.3 %attend.2 = (bf16[8,1024,128]{2,1,0:T(8,128)(2,1)}, f32[8,4,2,512]{3,2,1,0:T(2,128)}) custom-call(bf16[8,1024,128]{2,1,0:T(8,128)(2,1)} %get-tuple-element.80.q_ref, bf16[8,1024,128]{2,1,0:T(8,128)(2,1)} %get-tuple-element.81.k_ref, bf16[8,1024,128]{2,1,0:T(8,128)(2,1)} %get-tuple-element.82.v_ref), custom_call_target="tpu_custom_call" | custom-call | flops 17179869184 | bytes 16777216 | tf_op jit(solution)/shard_map/attend/pallas_call | solution.py:325
  47.0 7.2 %merge.2 = (bf16[1024,1024]{1,0:T(8,128)(2,1)}, bf16[1024,1024]{1,0:T(8,128)(2,1)}) custom-call(bf16[1024,1024]{1,0:T(8,128)(2,1)} %x_ref.6, bf16[1,1024]{1,0:T(2,128)(2,1)} %broadcast_in_dim.52.gain_ref, bf16[8,1024,128]{2,1,0:T(8,128)(2,1)} %get-tuple-element.83.ctx_ref, bf16[1024,1024]{1,0:T(8,128)(2,1)} %bitcast.51), custom_call_target="tpu_custom_call" | custom-call | flops 2147483648 | bytes 16777216 | tf_op jit(solution)/shard_map/merge/pallas_call | solution.py:327
  54.1 0.0 reduce-scatter.3.cloned.1.call-start
  54.2 0.1 iota_add_fusion
  54.3 0.1 add.37
  54.5 0.9 select_reduce_fusion.2
  55.4 0.1 stack.40
  55.5 0.1 stack.41
  55.6 1.2 select_reduce_fusion.3
  56.8 0.1 convert_element_type.48
  56.9 0.1 convert_element_type.51
  57.0 0.5 pad_maximum_fusion.1
  57.6 3.8 collective-permute-start.6
  61.3 0.6 collective-permute-start.5
  61.9 1.4 collective-permute-start.4
  63.3 0.3 collective-permute-start.3
  63.7 0.1 collective-permute-start
  63.8 9.8 %project.3 = (bf16[8,1024,128]{2,1,0:T(8,128)(2,1)}, bf16[8,1024,128]{2,1,0:T(8,128)(2,1)}, bf16[8,1024,128]{2,1,0:T(8,128)(2,1)}) custom-call(bf16[1024,1024]{1,0:T(8,128)(2,1)} %x_ref.9, bf16[1,1024]{1,0:T(2,128)(2,1)} %broadcast_in_dim.53.gain_ref, bf16[2048,1024]{1,0:T(8,128)(2,1)} %pad_maximum_fusion.w_ref), custom_call_target="tpu_custom_call" | custom-call | flops 4294967296 | bytes 16777216 | tf_op jit(solution)/shard_map/project/pallas_call | solution.py:308
  73.6 0.5 pad_add_fusion.order
  74.1 1.5 collective-permute-start.1
  75.7 4.6 collective-permute-done.1
  80.3 0.9 collective-permute-start.2
  81.2 4.8 collective-permute-done.2
  86.2 1.8 fusion.1
  88.0 14.4 %all-gather.3.cloned.1.call-done = bf16[8192,1024]{1,0:T(8,128)(2,1)} async-done(((bf16[1024,1024]{1,0:T(8,128)(2,1)}), bf16[8192,1024]{1,0:T(8,128)(2,1)}) %all-gather.3.cloned.1.call-update) | async-done | bytes 16777232 | tf_op jit(solution)/shard_map/all_gather | solution.py:424
  102.4 68.8 %experts_backward.2 = (f32[4,1024,1024]{2,1,0:T(8,128)}, bf16[4,2048,1024]{2,1,0:T(8,128)(2,1)}, bf16[4,2048,512]{2,1,0:T(8,128)(2,1)}, bf16[4,2048,512]{2,1,0:T(8,128)(2,1)}, bf16[4,2048,512]{2,1,0:T(8,128)(2,1)}) custom-call(s32[8,4]{1,0:T(8,128)} %get-tuple-element.149.counts, s32[2,8]{1,0:T(2,128)} %pad_add_fusion.order, f32[8,4,4,1024]{3,2,1,0:T(4,128)} %copy-done.1, ...), custom_call_target="tpu_custom_call" | custom-call | flops 38654705664 | bytes 16777216 | tf_op jit(solution)/shard_map/experts_backward/pallas_call | solution.py:164
  171.2 0.2 collective-permute-start.7
  171.5 71.1 %experts_backward.3 = (f32[4,1024,1024]{2,1,0:T(8,128)}, bf16[4,2048,1024]{2,1,0:T(8,128)(2,1)}, bf16[4,2048,512]{2,1,0:T(8,128)(2,1)}, bf16[4,2048,512]{2,1,0:T(8,128)(2,1)}, bf16[4,2048,512]{2,1,0:T(8,128)(2,1)}) custom-call(s32[8,4]{1,0:T(8,128)} %get-tuple-element.149.counts, s32[2,8]{1,0:T(2,128)} %pad_add_fusion.order, f32[8,4,4,1024]{3,2,1,0:T(4,128)} %copy-done.1, ...), custom_call_target="tpu_custom_call" | custom-call | flops 38654705664 | bytes 16777216 | tf_op jit(solution)/shard_map/experts_backward/pallas_call | solution.py:164
  242.5 17.0 %add.39 = f32[4,1024,1024]{2,1,0:T(8,128)} add(f32[4,1024,1024]{2,1,0:T(8,128)} %get-tuple-element.91, f32[4,1024,1024]{2,1,0:T(8,128)} %collective-permute-done.7) | non-fusion elementwise | flops 4194304 | bytes 50331648 | tf_op jit(solution)/shard_map/add | solution.py:438
  259.6 0.0 reduce-scatter.5.cloned.1.call-start
  259.7 57.2 %experts_forward.2 = f32[4,1024,1024]{2,1,0:T(8,128)} custom-call(s32[8,4]{1,0:T(8,128)} %get-tuple-element.150.counts, s32[2,8]{1,0:T(2,128)} %pad_add_fusion.order, f32[8,4,4,1024]{3,2,1,0:T(4,128)} %copy-done.1, bf16[8,1024,1024]{2,1,0:T(8,128)(2,1)} %bitcast.47, bf16[4,1024,512]{2,1,0:T(8,128)(2,1)} %w1_ref.7, bf16[4,1024,512]{2,1,0:T(8,128)(2,1)} %w3_ref.7, ...), custom_call_target="tpu_custom_call" | custom-call | flops 30064771072 | bytes 16777216 | tf_op jit(solution)/shard_map/experts_forward/pallas_call | solution.py:153
  316.8 0.2 collective-permute-start.8
  317.1 23.3 %attend.3 = (bf16[8,1024,128]{2,1,0:T(8,128)(2,1)}, f32[8,4,2,512]{3,2,1,0:T(2,128)}) custom-call(bf16[8,1024,128]{2,1,0:T(8,128)(2,1)} %get-tuple-element.104.q_ref, bf16[8,1024,128]{2,1,0:T(8,128)(2,1)} %get-tuple-element.105.k_ref, bf16[8,1024,128]{2,1,0:T(8,128)(2,1)} %get-tuple-element.106.v_ref), custom_call_target="tpu_custom_call" | custom-call | flops 17179869184 | bytes 16777216 | tf_op jit(solution)/shard_map/attend/pallas_call | solution.py:325
  340.4 7.1 %merge.3 = (bf16[1024,1024]{1,0:T(8,128)(2,1)}, bf16[1024,1024]{1,0:T(8,128)(2,1)}) custom-call(bf16[1024,1024]{1,0:T(8,128)(2,1)} %x_ref.9, bf16[1,1024]{1,0:T(2,128)(2,1)} %broadcast_in_dim.52.gain_ref, bf16[8,1024,128]{2,1,0:T(8,128)(2,1)} %get-tuple-element.107.ctx_ref, bf16[1024,1024]{1,0:T(8,128)(2,1)} %bitcast.52), custom_call_target="tpu_custom_call" | custom-call | flops 2147483648 | bytes 16777216 | tf_op jit(solution)/shard_map/merge/pallas_call | solution.py:327
  347.5 58.6 %experts_forward.3 = f32[4,1024,1024]{2,1,0:T(8,128)} custom-call(s32[8,4]{1,0:T(8,128)} %get-tuple-element.150.counts, s32[2,8]{1,0:T(2,128)} %pad_add_fusion.order, f32[8,4,4,1024]{3,2,1,0:T(4,128)} %copy-done.1, bf16[8,1024,1024]{2,1,0:T(8,128)(2,1)} %bitcast.48, bf16[4,1024,512]{2,1,0:T(8,128)(2,1)} %w1_ref.7, bf16[4,1024,512]{2,1,0:T(8,128)(2,1)} %w3_ref.7, ...), custom_call_target="tpu_custom_call" | custom-call | flops 30064771072 | bytes 16777216 | tf_op jit(solution)/shard_map/experts_forward/pallas_call | solution.py:153
  406.2 5.1 reduce-scatter.3.cloned.1.call-done.du_ref
  411.3 13.0 %out_pull.1 = (bf16[1024,1024]{1,0:T(8,128)(2,1)}, bf16[8,1024,128]{2,1,0:T(8,128)(2,1)}, f32[1024,1024]{1,0:T(8,128)}, f32[1,1024]{1,0:T(1,128)}) custom-call(bf16[1024,1024]{1,0:T(8,128)(2,1)} %get-tuple-element.116.h_ref, bf16[1024,1024]{1,0:T(8,128)(2,1)} %dy_ref.1, f32[1024,1024]{1,0:T(8,128)} %reduce-scatter.3.cloned.1.call-done.du_ref, ...), custom_call_target="tpu_custom_call" | custom-call | flops 4294967296 | bytes 16777216 | tf_op jit(solution)/shard_map/out_pull/pallas_call | solution.py:385
  424.2 38.7 %attend_pull.1 = (bf16[8,1024,128]{2,1,0:T(8,128)(2,1)}, bf16[8,1024,128]{2,1,0:T(8,128)(2,1)}, bf16[8,1024,128]{2,1,0:T(8,128)(2,1)}) custom-call(bf16[8,1024,128]{2,1,0:T(8,128)(2,1)} %get-tuple-element.104.q_ref, bf16[8,1024,128]{2,1,0:T(8,128)(2,1)} %get-tuple-element.105.k_ref, bf16[8,1024,128]{2,1,0:T(8,128)(2,1)} %get-tuple-element.106.v_ref, ...), custom_call_target="tpu_custom_call" | custom-call | flops 42949672960 | bytes 16777216 | tf_op jit(solution)/shard_map/attend_pull/pallas_call | solution.py:389
  462.9 17.7 %in_pull.1 = (bf16[1024,1024]{1,0:T(8,128)(2,1)}, f32[1024,1024]{1,0:T(8,128)}, f32[512,1024]{1,0:T(8,128)}, f32[512,1024]{1,0:T(8,128)}, f32[1,1024]{1,0:T(1,128)}) custom-call(bf16[1024,1024]{1,0:T(8,128)(2,1)} %x_ref.9, bf16[1024,1024]{1,0:T(8,128)(2,1)} %get-tuple-element.118.dh_ref, bf16[8,1024,128]{2,1,0:T(8,128)(2,1)} %get-tuple-element.121.dq_ref, ...), custom_call_target="tpu_custom_call" | custom-call | flops 8589934592 | bytes 16777216 | tf_op jit(solution)/shard_map/in_pull/pallas_call | solution.py:398
  480.7 71.9 %experts_weights.1 = (f32[4,1024,512]{2,1,0:T(8,128)}, f32[4,512,1024]{2,1,0:T(8,128)}, f32[4,1024,512]{2,1,0:T(8,128)}) custom-call(s32[8,4]{1,0:T(8,128)} %get-tuple-element.149.counts, s32[2,8]{1,0:T(2,128)} %pad_add_fusion.order, bf16[4,4096,1024]{2,1,0:T(8,128)(2,1)} %refs_5_.1, bf16[4,2048,1024]{2,1,0:T(8,128)(2,1)} %get-tuple-element.129.refs_1_, ...), custom_call_target="tpu_custom_call" | custom-call | flops 25769803776 | bytes 16777216 | tf_op jit(solution)/shard_map/experts_weights/pallas_call | solution.py:177
  552.6 9.5 %reduce-scatter.5.cloned.1.call-done = f32[1024,1024]{1,0:T(8,128)} async-done(((f32[4096,1024]{1,0:T(8,128)}), f32[1024,1024]{1,0:T(8,128)}) %reduce-scatter.5.cloned.1.call-update) | async-done | bytes 4194320 | tf_op jit(solution)/shard_map/reduce_scatter | solution.py:433
  562.1 4.3 add_convert_fusion
  (44 shorter events, 0.3 us)
Async XLA Ops:
  7.2 95.2 %all-gather.3.cloned.1.call-start = ((), (), s32[]{:S(2)}) async-start(), calls=%async_computation.2 | async-start | bytes 18874368 | tf_op jit(solution)/shard_map/all_gather | solution.py:424
  7.9 251.7 %all-gather.5.cloned.1.call-start = ((), (), s32[]{:S(2)}) async-start(), calls=%async_computation.3 | async-start | bytes 18874368 | tf_op jit(solution)/shard_map/all_gather | solution.py:430
  46.9 7.5 %copy-start.6 = (bf16[1024,8]{0,1:T(8,128)(2,1)S(1)}, bf16[1024,8]{0,1:T(8,128)(2,1)}, u32[]{:S(2)}) copy-start(bf16[1024,8]{0,1:T(8,128)(2,1)} %param.24) | copy-start | bytes 49156
  46.9 7.5 %copy-start.7 = (bf16[1024,8]{0,1:T(8,128)(2,1)S(1)}, bf16[1024,8]{0,1:T(8,128)(2,1)}, u32[]{:S(2)}) copy-start(bf16[1024,8]{0,1:T(8,128)(2,1)} %param.27) | copy-start | bytes 49156
  46.9 7.5 %copy-start.4 = (s32[1024,8]{0,1:T(8,128)S(1)}, s32[1024,8]{0,1:T(8,128)}, u32[]{:S(2)}) copy-start(s32[1024,8]{0,1:T(8,128)} %param.26) | copy-start | bytes 98308
  46.9 7.5 %copy-start.5 = (s32[1024,8]{0,1:T(8,128)S(1)}, s32[1024,8]{0,1:T(8,128)}, u32[]{:S(2)}) copy-start(s32[1024,8]{0,1:T(8,128)} %param.23) | copy-start | bytes 98308
  46.9 7.5 %copy-start.2 = (s32[1024,8]{0,1:T(8,128)S(1)}, s32[1024,8]{0,1:T(8,128)}, u32[]{:S(2)}) copy-start(s32[1024,8]{0,1:T(8,128)} %param.22) | copy-start | bytes 98308
  47.0 7.5 %copy-start.3 = (s32[1024,8]{0,1:T(8,128)S(1)}, s32[1024,8]{0,1:T(8,128)}, u32[]{:S(2)}) copy-start(s32[1024,8]{0,1:T(8,128)} %param.25) | copy-start | bytes 98308
  54.1 357.1 %reduce-scatter.3.cloned.1.call-start = ((), (), s32[]{:S(2)}) async-start(), calls=%async_computation.4 | async-start | bytes 20971520 | tf_op jit(solution)/shard_map/reduce_scatter | solution.py:433
  57.6 28.6 %collective-permute-start.6 = (f32[4,4,1024]{2,1,0:T(4,128)S(1)}, f32[4,4,1024]{2,1,0:T(4,128)S(1)}, u32[]{:S(2)}, u32[]{:S(2)}) collective-permute-start(f32[4,4,1024]{2,1,0:T(4,128)S(1)} %get-tuple-element.155), channel_id=1, source_target_pairs={{0,7},{1,6},{2,5},{3,4},{4,3},{5,2},{6,1},{7,0}} | collective-permute-start | bytes 196616 | tf_op jit(solution)/shard_map/ppermute | solution.py:21
  61.3 24.8 %collective-permute-start.5 = (f32[4,4,1024]{2,1,0:T(4,128)S(1)}, f32[4,4,1024]{2,1,0:T(4,128)S(1)}, u32[]{:S(2)}, u32[]{:S(2)}) collective-permute-start(f32[4,4,1024]{2,1,0:T(4,128)S(1)} %get-tuple-element.156), channel_id=1, source_target_pairs={{0,6},{1,7},{2,4},{3,5},{4,2},{5,3},{6,0},{7,1}} | collective-permute-start | bytes 196616 | tf_op jit(solution)/shard_map/ppermute | solution.py:21
  61.9 24.1 %collective-permute-start.4 = (f32[4,4,1024]{2,1,0:T(4,128)S(1)}, f32[4,4,1024]{2,1,0:T(4,128)S(1)}, u32[]{:S(2)}, u32[]{:S(2)}) collective-permute-start(f32[4,4,1024]{2,1,0:T(4,128)S(1)} %get-tuple-element.157), channel_id=1, source_target_pairs={{0,5},{1,4},{2,7},{3,6},{4,1},{5,0},{6,3},{7,2}} | collective-permute-start | bytes 196616 | tf_op jit(solution)/shard_map/ppermute | solution.py:21
  63.3 22.7 %collective-permute-start.3 = (f32[4,4,1024]{2,1,0:T(4,128)S(1)}, f32[4,4,1024]{2,1,0:T(4,128)S(1)}, u32[]{:S(2)}, u32[]{:S(2)}) collective-permute-start(f32[4,4,1024]{2,1,0:T(4,128)S(1)} %get-tuple-element.158), channel_id=1, source_target_pairs={{0,4},{1,5},{2,6},{3,7},{4,0},{5,1},{6,2},{7,3}} | collective-permute-start | bytes 196616 | tf_op jit(solution)/shard_map/ppermute | solution.py:21
  63.7 10.5 %collective-permute-start = (f32[4,4,1024]{2,1,0:T(4,128)S(1)}, f32[4,4,1024]{2,1,0:T(4,128)S(1)}, u32[]{:S(2)}, u32[]{:S(2)}) collective-permute-start(f32[4,4,1024]{2,1,0:T(4,128)S(1)} %get-tuple-element.161), channel_id=1, source_target_pairs={{0,1},{1,0},{2,3},{3,2},{4,5},{5,4},{6,7},{7,6}} | collective-permute-start | bytes 196616 | tf_op jit(solution)/shard_map/ppermute | solution.py:21
  74.1 6.2 %collective-permute-start.1 = (f32[4,4,1024]{2,1,0:T(4,128)S(1)}, f32[4,4,1024]{2,1,0:T(4,128)S(1)}, u32[]{:S(2)}, u32[]{:S(2)}) collective-permute-start(f32[4,4,1024]{2,1,0:T(4,128)S(1)} %get-tuple-element.160), channel_id=1, source_target_pairs={{0,2},{1,3},{2,0},{3,1},{4,6},{5,7},{6,4},{7,5}} | collective-permute-start | bytes 196616 | tf_op jit(solution)/shard_map/ppermute | solution.py:21
  80.3 5.7 %collective-permute-start.2 = (f32[4,4,1024]{2,1,0:T(4,128)S(1)}, f32[4,4,1024]{2,1,0:T(4,128)S(1)}, u32[]{:S(2)}, u32[]{:S(2)}) collective-permute-start(f32[4,4,1024]{2,1,0:T(4,128)S(1)} %get-tuple-element.159), channel_id=1, source_target_pairs={{0,3},{1,2},{2,1},{3,0},{4,7},{5,6},{6,5},{7,4}} | collective-permute-start | bytes 196616 | tf_op jit(solution)/shard_map/ppermute | solution.py:21
  86.2 16.2 %copy-start.1 = (f32[8,4,4,1024]{3,2,1,0:T(4,128)}, f32[8,4,4,1024]{3,2,1,0:T(4,128)S(1)}, u32[]{:S(2)}) copy-start(f32[8,4,4,1024]{3,2,1,0:T(4,128)S(1)} %bitcast_dynamic-update-slice_fusion.meta_ref) | copy-start | bytes 1572868
  171.2 71.3 %collective-permute-start.7 = (f32[4,1024,1024]{2,1,0:T(8,128)}, f32[4,1024,1024]{2,1,0:T(8,128)}, u32[]{:S(2)}, u32[]{:S(2)}) collective-permute-start(f32[4,1024,1024]{2,1,0:T(8,128)} %get-tuple-element.92), channel_id=1, source_target_pairs={{0,1},{1,0},{2,3},{3,2},{4,5},{5,4},{6,7},{7,6}} | collective-permute-start | bytes 50331656 | tf_op jit(solution)/shard_map/ppermute | solution.py:21
  259.6 302.5 %reduce-scatter.5.cloned.1.call-start = ((), (), s32[]{:S(2)}) async-start(), calls=%async_computation.5 | async-start | bytes 20971520 | tf_op jit(solution)/shard_map/reduce_scatter | solution.py:433
  316.8 30.7 %collective-permute-start.8 = (f32[4,1024,1024]{2,1,0:T(8,128)}, f32[4,1024,1024]{2,1,0:T(8,128)}, u32[]{:S(2)}, u32[]{:S(2)}) collective-permute-start(f32[4,1024,1024]{2,1,0:T(8,128)} %experts_forward.2), channel_id=1, source_target_pairs={{0,1},{1,0},{2,3},{3,2},{4,5},{5,4},{6,7},{7,6}} | collective-permute-start | bytes 50331656 | tf_op jit(solution)/shard_map/ppermute | solution.py:21
  480.7 81.4 %copy-start = (bf16[1024,1024]{1,0:T(8,128)(2,1)S(1)}, bf16[1024,1024]{1,0:T(8,128)(2,1)}, u32[]{:S(2)}) copy-start(bf16[1024,1024]{1,0:T(8,128)(2,1)} %get-tuple-element.84) | copy-start | bytes 6291460
Sparse Core Ops, SparseCore 0:
  9.8 92.5 all-gather.2
  104.8 85.2 all-gather.4
  259.7 151.4 reduce-scatter.2
  414.1 147.9 reduce-scatter.4

commit v3 on v2

--- a/solution.py
+++ b/solution.py
@@ -35,7 +35,7 @@
 
 
 def fill_sizes(capacity):
-    return (capacity * 17 // 32 // 16 * 16, capacity)
+    return (capacity // 2, capacity * 9 // 16 // 16 * 16, capacity)
 
 
 def by_fill(count, capacity, body):

time: 580 us -> 564 us (0.972)
  Pallas kernels: 477 us -> 420 us
  waiting for transfers between devices: 39.1 us -> 70.3 us
  starting transfers between devices: 9.38 us -> 17.2 us
    reduce_scatter x2, waiting for transfers between devices: 14.6 us -> 45.5 us  [local_step(): lax.psum_scatter(part.reshape(-1, model_dim), 'expert', scatter_dimension...]
    pallas_call x2, Pallas kernels: 140 us -> 119 us  [experts_backward(): ordered_call(functools.partial(backward_kernel, capacity, bit), 'experts_...]
    pallas_call x2, Pallas kernels: 116 us -> 96.8 us  [experts_forward(): ordered_call(functools.partial(forward_kernel, capacity, bit), 'experts_f...]
    pallas_call x1, Pallas kernels: 71.9 us -> 55.8 us  [experts_weights(): ordered_call(functools.partial(weights_kernel, capacity), 'experts_weight...]
    ppermute x9, starting transfers between devices: 9.23 us -> 17.1 us  [swap(): return lax.ppermute(values, 'expert', [(i, i ^ mask) for i in range(group)])]
  transfers between devices with their start and end apart: 13 -> 13, of which waited for: 5 -> 5; matrix products, arithmetic and copies ran while one was open for 5% -> 5% of each run, Pallas kernels for 83% -> 76%
where the time goes in v3:
time: 564 us; the launch traced here: 555 us
  Pallas kernels  420 us (74%)
  waiting for transfers between devices  70.3 us (12%)
  other arithmetic  30.1 us (5%)
  starting transfers between devices  17.2 us (3%)
  between operations  14.2 us (3%)
    pallas_call x2, Pallas kernels, experts_backward(): ordered_call(functools.partial(backward_kernel, capacity, bit), 'experts_...  119 us
    pallas_call x2, Pallas kernels, experts_forward(): ordered_call(functools.partial(forward_kernel, capacity, bit), 'experts_f...  96.8 us
    pallas_call x1, Pallas kernels, experts_weights(): ordered_call(functools.partial(weights_kernel, capacity), 'experts_weight...  55.8 us
    pallas_call x2, Pallas kernels, attention_forward(): call(functools.partial(attend_kernel, block), 'attend', (heads, jax.Shape...  46.6 us
    reduce_scatter x2, waiting for transfers between devices, local_step(): lax.psum_scatter(part.reshape(-1, model_dim), 'expert', scatter_dimension...  45.5 us
    pallas_call x1, Pallas kernels, attention_pull(): call(functools.partial(attend_pull_kernel, tokens // 4, (width // 2) ** (...  38.5 us
    pallas_call x2, Pallas kernels, project(): call(functools.partial(project_kernel, (width // 2) ** (-0.5)), 'project'...  18.9 us
    pallas_call x1, Pallas kernels, projection_pull(): call(in_pull_kernel, 'in_pull', (like, wide(model_dim, model_dim), wide(m...  17.7 us
  transfers between devices with their start and end apart: 13, of which 5 were waited for; matrix products, arithmetic and copies ran while one was open for 5% of the time, Pallas kernels for 76%

profile of v3, /device:TPU:0, one launch (start us, length us, event | category | flops | bytes accessed | tf_op | source)
XLA Modules:
  0.0 555.4 jit_solution(15394358850953755258)
XLA Ops:
  7.2 0.7 all-gather.3.cloned.1.call-update
  7.9 0.0 all-gather.5.cloned.1.call-start
  8.0 1.3 broadcast_in_dim.53.gain_ref
  9.2 1.3 broadcast_in_dim.52.gain_ref
  10.5 3.7 pad_maximum_fusion.w_ref
  14.2 9.4 %project.2 = (bf16[8,1024,128]{2,1,0:T(8,128)(2,1)}, bf16[8,1024,128]{2,1,0:T(8,128)(2,1)}, bf16[8,1024,128]{2,1,0:T(8,128)(2,1)}) custom-call(bf16[1024,1024]{1,0:T(8,128)(2,1)} %x_ref.6, bf16[1,1024]{1,0:T(2,128)(2,1)} %broadcast_in_dim.53.gain_ref, bf16[2048,1024]{1,0:T(8,128)(2,1)} %pad_maximum_fusion.w_ref), custom_call_target="tpu_custom_call" | custom-call | flops 4294967296 | bytes 16777216 | tf_op jit(solution)/shard_map/project/pallas_call | solution.py:308
  23.6 23.3 %attend.2 = (bf16[8,1024,128]{2,1,0:T(8,128)(2,1)}, f32[8,4,2,512]{3,2,1,0:T(2,128)}) custom-call(bf16[8,1024,128]{2,1,0:T(8,128)(2,1)} %get-tuple-element.80.q_ref, bf16[8,1024,128]{2,1,0:T(8,128)(2,1)} %get-tuple-element.81.k_ref, bf16[8,1024,128]{2,1,0:T(8,128)(2,1)} %get-tuple-element.82.v_ref), custom_call_target="tpu_custom_call" | custom-call | flops 17179869184 | bytes 16777216 | tf_op jit(solution)/shard_map/attend/pallas_call | solution.py:325
  47.0 7.2 %merge.2 = (bf16[1024,1024]{1,0:T(8,128)(2,1)}, bf16[1024,1024]{1,0:T(8,128)(2,1)}) custom-call(bf16[1024,1024]{1,0:T(8,128)(2,1)} %x_ref.6, bf16[1,1024]{1,0:T(2,128)(2,1)} %broadcast_in_dim.52.gain_ref, bf16[8,1024,128]{2,1,0:T(8,128)(2,1)} %get-tuple-element.83.ctx_ref, bf16[1024,1024]{1,0:T(8,128)(2,1)} %bitcast.51), custom_call_target="tpu_custom_call" | custom-call | flops 2147483648 | bytes 16777216 | tf_op jit(solution)/shard_map/merge/pallas_call | solution.py:327
  54.1 0.0 reduce-scatter.3.cloned.1.call-start
  54.2 0.1 iota_add_fusion
  54.3 0.1 add.37
  54.5 0.9 select_reduce_fusion.2
  55.4 0.1 stack.40
  55.5 0.1 stack.41
  55.6 1.2 select_reduce_fusion.3
  56.8 0.1 convert_element_type.48
  56.9 0.1 convert_element_type.51
  57.0 0.5 pad_maximum_fusion.1
  57.6 3.8 collective-permute-start.6
  61.3 0.6 collective-permute-start.5
  61.9 1.4 collective-permute-start.4
  63.3 0.3 collective-permute-start.3
  63.6 0.1 collective-permute-start
  63.8 9.5 %project.3 = (bf16[8,1024,128]{2,1,0:T(8,128)(2,1)}, bf16[8,1024,128]{2,1,0:T(8,128)(2,1)}, bf16[8,1024,128]{2,1,0:T(8,128)(2,1)}) custom-call(bf16[1024,1024]{1,0:T(8,128)(2,1)} %x_ref.9, bf16[1,1024]{1,0:T(2,128)(2,1)} %broadcast_in_dim.53.gain_ref, bf16[2048,1024]{1,0:T(8,128)(2,1)} %pad_maximum_fusion.w_ref), custom_call_target="tpu_custom_call" | custom-call | flops 4294967296 | bytes 16777216 | tf_op jit(solution)/shard_map/project/pallas_call | solution.py:308
  73.3 0.5 pad_add_fusion.order
  73.8 1.5 collective-permute-start.1
  75.4 4.6 collective-permute-done.1
  80.0 1.0 collective-permute-start.2
  81.0 4.7 collective-permute-done.2
  85.9 1.8 fusion.1
  87.7 14.7 %all-gather.3.cloned.1.call-done = bf16[8192,1024]{1,0:T(8,128)(2,1)} async-done(((bf16[1024,1024]{1,0:T(8,128)(2,1)}), bf16[8192,1024]{1,0:T(8,128)(2,1)}) %all-gather.3.cloned.1.call-update) | async-done | bytes 16777232 | tf_op jit(solution)/shard_map/all_gather | solution.py:424
  102.4 58.6 %experts_backward.2 = (f32[4,1024,1024]{2,1,0:T(8,128)}, bf16[4,2048,1024]{2,1,0:T(8,128)(2,1)}, bf16[4,2048,512]{2,1,0:T(8,128)(2,1)}, bf16[4,2048,512]{2,1,0:T(8,128)(2,1)}, bf16[4,2048,512]{2,1,0:T(8,128)(2,1)}) custom-call(s32[8,4]{1,0:T(8,128)} %get-tuple-element.149.counts, s32[2,8]{1,0:T(2,128)} %pad_add_fusion.order, f32[8,4,4,1024]{3,2,1,0:T(4,128)} %copy-done.1, ...), custom_call_target="tpu_custom_call" | custom-call | flops 38654705664 | bytes 16777216 | tf_op jit(solution)/shard_map/experts_backward/pallas_call | solution.py:164
  161.0 6.4 %collective-permute-start.7 = (f32[4,1024,1024]{2,1,0:T(8,128)}, f32[4,1024,1024]{2,1,0:T(8,128)}, u32[]{:S(2)}, u32[]{:S(2)}) collective-permute-start(f32[4,1024,1024]{2,1,0:T(8,128)} %get-tuple-element.92), channel_id=1, source_target_pairs={{0,1},{1,0},{2,3},{3,2},{4,5},{5,4},{6,7},{7,6}} | collective-permute-start | bytes 50331656 | tf_op jit(solution)/shard_map/ppermute | solution.py:21
  167.4 60.1 %experts_backward.3 = (f32[4,1024,1024]{2,1,0:T(8,128)}, bf16[4,2048,1024]{2,1,0:T(8,128)(2,1)}, bf16[4,2048,512]{2,1,0:T(8,128)(2,1)}, bf16[4,2048,512]{2,1,0:T(8,128)(2,1)}, bf16[4,2048,512]{2,1,0:T(8,128)(2,1)}) custom-call(s32[8,4]{1,0:T(8,128)} %get-tuple-element.149.counts, s32[2,8]{1,0:T(2,128)} %pad_add_fusion.order, f32[8,4,4,1024]{3,2,1,0:T(4,128)} %copy-done.1, ...), custom_call_target="tpu_custom_call" | custom-call | flops 38654705664 | bytes 16777216 | tf_op jit(solution)/shard_map/experts_backward/pallas_call | solution.py:164
  227.5 17.0 %add.39 = f32[4,1024,1024]{2,1,0:T(8,128)} add(f32[4,1024,1024]{2,1,0:T(8,128)} %get-tuple-element.91, f32[4,1024,1024]{2,1,0:T(8,128)} %collective-permute-done.7) | non-fusion elementwise | flops 4194304 | bytes 50331648 | tf_op jit(solution)/shard_map/add | solution.py:438
  244.5 0.0 reduce-scatter.5.cloned.1.call-start
  244.6 47.4 %experts_forward.2 = f32[4,1024,1024]{2,1,0:T(8,128)} custom-call(s32[8,4]{1,0:T(8,128)} %get-tuple-element.150.counts, s32[2,8]{1,0:T(2,128)} %pad_add_fusion.order, f32[8,4,4,1024]{3,2,1,0:T(4,128)} %copy-done.1, bf16[8,1024,1024]{2,1,0:T(8,128)(2,1)} %bitcast.47, bf16[4,1024,512]{2,1,0:T(8,128)(2,1)} %w1_ref.7, bf16[4,1024,512]{2,1,0:T(8,128)(2,1)} %w3_ref.7, ...), custom_call_target="tpu_custom_call" | custom-call | flops 30064771072 | bytes 16777216 | tf_op jit(solution)/shard_map/experts_forward/pallas_call | solution.py:153
  292.0 1.9 collective-permute-start.8
  293.9 23.3 %attend.3 = (bf16[8,1024,128]{2,1,0:T(8,128)(2,1)}, f32[8,4,2,512]{3,2,1,0:T(2,128)}) custom-call(bf16[8,1024,128]{2,1,0:T(8,128)(2,1)} %get-tuple-element.104.q_ref, bf16[8,1024,128]{2,1,0:T(8,128)(2,1)} %get-tuple-element.105.k_ref, bf16[8,1024,128]{2,1,0:T(8,128)(2,1)} %get-tuple-element.106.v_ref), custom_call_target="tpu_custom_call" | custom-call | flops 17179869184 | bytes 16777216 | tf_op jit(solution)/shard_map/attend/pallas_call | solution.py:325
  317.2 7.1 %merge.3 = (bf16[1024,1024]{1,0:T(8,128)(2,1)}, bf16[1024,1024]{1,0:T(8,128)(2,1)}) custom-call(bf16[1024,1024]{1,0:T(8,128)(2,1)} %x_ref.9, bf16[1,1024]{1,0:T(2,128)(2,1)} %broadcast_in_dim.52.gain_ref, bf16[8,1024,128]{2,1,0:T(8,128)(2,1)} %get-tuple-element.107.ctx_ref, bf16[1024,1024]{1,0:T(8,128)(2,1)} %bitcast.52), custom_call_target="tpu_custom_call" | custom-call | flops 2147483648 | bytes 16777216 | tf_op jit(solution)/shard_map/merge/pallas_call | solution.py:327
  324.3 49.5 %experts_forward.3 = f32[4,1024,1024]{2,1,0:T(8,128)} custom-call(s32[8,4]{1,0:T(8,128)} %get-tuple-element.150.counts, s32[2,8]{1,0:T(2,128)} %pad_add_fusion.order, f32[8,4,4,1024]{3,2,1,0:T(4,128)} %copy-done.1, bf16[8,1024,1024]{2,1,0:T(8,128)(2,1)} %bitcast.48, bf16[4,1024,512]{2,1,0:T(8,128)(2,1)} %w1_ref.7, bf16[4,1024,512]{2,1,0:T(8,128)(2,1)} %w3_ref.7, ...), custom_call_target="tpu_custom_call" | custom-call | flops 30064771072 | bytes 16777216 | tf_op jit(solution)/shard_map/experts_forward/pallas_call | solution.py:153
  373.8 19.8 %reduce-scatter.3.cloned.1.call-done.du_ref = f32[1024,1024]{1,0:T(8,128)} async-done(((f32[4096,1024]{1,0:T(8,128)}), f32[1024,1024]{1,0:T(8,128)}) %reduce-scatter.3.cloned.1.call-update) | async-done | bytes 4194320 | tf_op jit(solution)/shard_map/reduce_scatter | solution.py:433
  393.6 13.0 %out_pull.1 = (bf16[1024,1024]{1,0:T(8,128)(2,1)}, bf16[8,1024,128]{2,1,0:T(8,128)(2,1)}, f32[1024,1024]{1,0:T(8,128)}, f32[1,1024]{1,0:T(1,128)}) custom-call(bf16[1024,1024]{1,0:T(8,128)(2,1)} %get-tuple-element.116.h_ref, bf16[1024,1024]{1,0:T(8,128)(2,1)} %dy_ref.1, f32[1024,1024]{1,0:T(8,128)} %reduce-scatter.3.cloned.1.call-done.du_ref, ...), custom_call_target="tpu_custom_call" | custom-call | flops 4294967296 | bytes 16777216 | tf_op jit(solution)/shard_map/out_pull/pallas_call | solution.py:385
  406.6 38.5 %attend_pull.1 = (bf16[8,1024,128]{2,1,0:T(8,128)(2,1)}, bf16[8,1024,128]{2,1,0:T(8,128)(2,1)}, bf16[8,1024,128]{2,1,0:T(8,128)(2,1)}) custom-call(bf16[8,1024,128]{2,1,0:T(8,128)(2,1)} %get-tuple-element.104.q_ref, bf16[8,1024,128]{2,1,0:T(8,128)(2,1)} %get-tuple-element.105.k_ref, bf16[8,1024,128]{2,1,0:T(8,128)(2,1)} %get-tuple-element.106.v_ref, ...), custom_call_target="tpu_custom_call" | custom-call | flops 42949672960 | bytes 16777216 | tf_op jit(solution)/shard_map/attend_pull/pallas_call | solution.py:389
  445.1 17.7 %in_pull.1 = (bf16[1024,1024]{1,0:T(8,128)(2,1)}, f32[1024,1024]{1,0:T(8,128)}, f32[512,1024]{1,0:T(8,128)}, f32[512,1024]{1,0:T(8,128)}, f32[1,1024]{1,0:T(1,128)}) custom-call(bf16[1024,1024]{1,0:T(8,128)(2,1)} %x_ref.9, bf16[1024,1024]{1,0:T(8,128)(2,1)} %get-tuple-element.118.dh_ref, bf16[8,1024,128]{2,1,0:T(8,128)(2,1)} %get-tuple-element.121.dq_ref, ...), custom_call_target="tpu_custom_call" | custom-call | flops 8589934592 | bytes 16777216 | tf_op jit(solution)/shard_map/in_pull/pallas_call | solution.py:398
  462.9 55.8 %experts_weights.1 = (f32[4,1024,512]{2,1,0:T(8,128)}, f32[4,512,1024]{2,1,0:T(8,128)}, f32[4,1024,512]{2,1,0:T(8,128)}) custom-call(s32[8,4]{1,0:T(8,128)} %get-tuple-element.149.counts, s32[2,8]{1,0:T(2,128)} %pad_add_fusion.order, bf16[4,4096,1024]{2,1,0:T(8,128)(2,1)} %refs_5_.1, bf16[4,2048,1024]{2,1,0:T(8,128)(2,1)} %get-tuple-element.129.refs_1_, ...), custom_call_target="tpu_custom_call" | custom-call | flops 25769803776 | bytes 16777216 | tf_op jit(solution)/shard_map/experts_weights/pallas_call | solution.py:177
  518.7 25.7 %reduce-scatter.5.cloned.1.call-done = f32[1024,1024]{1,0:T(8,128)} async-done(((f32[4096,1024]{1,0:T(8,128)}), f32[1024,1024]{1,0:T(8,128)}) %reduce-scatter.5.cloned.1.call-update) | async-done | bytes 4194320 | tf_op jit(solution)/shard_map/reduce_scatter | solution.py:433
  544.5 4.3 add_convert_fusion
  (44 shorter events, 0.3 us)
Async XLA Ops:
  7.2 95.2 %all-gather.3.cloned.1.call-start = ((), (), s32[]{:S(2)}) async-start(), calls=%async_computation.2 | async-start | bytes 18874368 | tf_op jit(solution)/shard_map/all_gather | solution.py:424
  7.9 236.6 %all-gather.5.cloned.1.call-start = ((), (), s32[]{:S(2)}) async-start(), calls=%async_computation.3 | async-start | bytes 18874368 | tf_op jit(solution)/shard_map/all_gather | solution.py:430
  46.9 7.5 %copy-start.6 = (bf16[1024,8]{0,1:T(8,128)(2,1)S(1)}, bf16[1024,8]{0,1:T(8,128)(2,1)}, u32[]{:S(2)}) copy-start(bf16[1024,8]{0,1:T(8,128)(2,1)} %param.24) | copy-start | bytes 49156
  46.9 7.5 %copy-start.7 = (bf16[1024,8]{0,1:T(8,128)(2,1)S(1)}, bf16[1024,8]{0,1:T(8,128)(2,1)}, u32[]{:S(2)}) copy-start(bf16[1024,8]{0,1:T(8,128)(2,1)} %param.27) | copy-start | bytes 49156
  46.9 7.5 %copy-start.4 = (s32[1024,8]{0,1:T(8,128)S(1)}, s32[1024,8]{0,1:T(8,128)}, u32[]{:S(2)}) copy-start(s32[1024,8]{0,1:T(8,128)} %param.26) | copy-start | bytes 98308
  46.9 7.5 %copy-start.5 = (s32[1024,8]{0,1:T(8,128)S(1)}, s32[1024,8]{0,1:T(8,128)}, u32[]{:S(2)}) copy-start(s32[1024,8]{0,1:T(8,128)} %param.23) | copy-start | bytes 98308
  46.9 7.5 %copy-start.2 = (s32[1024,8]{0,1:T(8,128)S(1)}, s32[1024,8]{0,1:T(8,128)}, u32[]{:S(2)}) copy-start(s32[1024,8]{0,1:T(8,128)} %param.22) | copy-start | bytes 98308
  47.0 7.5 %copy-start.3 = (s32[1024,8]{0,1:T(8,128)S(1)}, s32[1024,8]{0,1:T(8,128)}, u32[]{:S(2)}) copy-start(s32[1024,8]{0,1:T(8,128)} %param.25) | copy-start | bytes 98308
  54.1 339.5 %reduce-scatter.3.cloned.1.call-start = ((), (), s32[]{:S(2)}) async-start(), calls=%async_computation.4 | async-start | bytes 20971520 | tf_op jit(solution)/shard_map/reduce_scatter | solution.py:433
  57.6 28.2 %collective-permute-start.6 = (f32[4,4,1024]{2,1,0:T(4,128)S(1)}, f32[4,4,1024]{2,1,0:T(4,128)S(1)}, u32[]{:S(2)}, u32[]{:S(2)}) collective-permute-start(f32[4,4,1024]{2,1,0:T(4,128)S(1)} %get-tuple-element.155), channel_id=1, source_target_pairs={{0,7},{1,6},{2,5},{3,4},{4,3},{5,2},{6,1},{7,0}} | collective-permute-start | bytes 196616 | tf_op jit(solution)/shard_map/ppermute | solution.py:21
  61.3 24.5 %collective-permute-start.5 = (f32[4,4,1024]{2,1,0:T(4,128)S(1)}, f32[4,4,1024]{2,1,0:T(4,128)S(1)}, u32[]{:S(2)}, u32[]{:S(2)}) collective-permute-start(f32[4,4,1024]{2,1,0:T(4,128)S(1)} %get-tuple-element.156), channel_id=1, source_target_pairs={{0,6},{1,7},{2,4},{3,5},{4,2},{5,3},{6,0},{7,1}} | collective-permute-start | bytes 196616 | tf_op jit(solution)/shard_map/ppermute | solution.py:21
  61.9 23.8 %collective-permute-start.4 = (f32[4,4,1024]{2,1,0:T(4,128)S(1)}, f32[4,4,1024]{2,1,0:T(4,128)S(1)}, u32[]{:S(2)}, u32[]{:S(2)}) collective-permute-start(f32[4,4,1024]{2,1,0:T(4,128)S(1)} %get-tuple-element.157), channel_id=1, source_target_pairs={{0,5},{1,4},{2,7},{3,6},{4,1},{5,0},{6,3},{7,2}} | collective-permute-start | bytes 196616 | tf_op jit(solution)/shard_map/ppermute | solution.py:21
  63.3 22.4 %collective-permute-start.3 = (f32[4,4,1024]{2,1,0:T(4,128)S(1)}, f32[4,4,1024]{2,1,0:T(4,128)S(1)}, u32[]{:S(2)}, u32[]{:S(2)}) collective-permute-start(f32[4,4,1024]{2,1,0:T(4,128)S(1)} %get-tuple-element.158), channel_id=1, source_target_pairs={{0,4},{1,5},{2,6},{3,7},{4,0},{5,1},{6,2},{7,3}} | collective-permute-start | bytes 196616 | tf_op jit(solution)/shard_map/ppermute | solution.py:21
  63.6 10.2 %collective-permute-start = (f32[4,4,1024]{2,1,0:T(4,128)S(1)}, f32[4,4,1024]{2,1,0:T(4,128)S(1)}, u32[]{:S(2)}, u32[]{:S(2)}) collective-permute-start(f32[4,4,1024]{2,1,0:T(4,128)S(1)} %get-tuple-element.161), channel_id=1, source_target_pairs={{0,1},{1,0},{2,3},{3,2},{4,5},{5,4},{6,7},{7,6}} | collective-permute-start | bytes 196616 | tf_op jit(solution)/shard_map/ppermute | solution.py:21
  73.8 6.2 %collective-permute-start.1 = (f32[4,4,1024]{2,1,0:T(4,128)S(1)}, f32[4,4,1024]{2,1,0:T(4,128)S(1)}, u32[]{:S(2)}, u32[]{:S(2)}) collective-permute-start(f32[4,4,1024]{2,1,0:T(4,128)S(1)} %get-tuple-element.160), channel_id=1, source_target_pairs={{0,2},{1,3},{2,0},{3,1},{4,6},{5,7},{6,4},{7,5}} | collective-permute-start | bytes 196616 | tf_op jit(solution)/shard_map/ppermute | solution.py:21
  80.0 5.7 %collective-permute-start.2 = (f32[4,4,1024]{2,1,0:T(4,128)S(1)}, f32[4,4,1024]{2,1,0:T(4,128)S(1)}, u32[]{:S(2)}, u32[]{:S(2)}) collective-permute-start(f32[4,4,1024]{2,1,0:T(4,128)S(1)} %get-tuple-element.159), channel_id=1, source_target_pairs={{0,3},{1,2},{2,1},{3,0},{4,7},{5,6},{6,5},{7,4}} | collective-permute-start | bytes 196616 | tf_op jit(solution)/shard_map/ppermute | solution.py:21
  85.8 16.5 %copy-start.1 = (f32[8,4,4,1024]{3,2,1,0:T(4,128)}, f32[8,4,4,1024]{3,2,1,0:T(4,128)S(1)}, u32[]{:S(2)}) copy-start(f32[8,4,4,1024]{3,2,1,0:T(4,128)S(1)} %bitcast_dynamic-update-slice_fusion.meta_ref) | copy-start | bytes 1572868
  161.0 66.5 %collective-permute-start.7 = (f32[4,1024,1024]{2,1,0:T(8,128)}, f32[4,1024,1024]{2,1,0:T(8,128)}, u32[]{:S(2)}, u32[]{:S(2)}) collective-permute-start(f32[4,1024,1024]{2,1,0:T(8,128)} %get-tuple-element.92), channel_id=1, source_target_pairs={{0,1},{1,0},{2,3},{3,2},{4,5},{5,4},{6,7},{7,6}} | collective-permute-start | bytes 50331656 | tf_op jit(solution)/shard_map/ppermute | solution.py:21
  244.5 299.9 %reduce-scatter.5.cloned.1.call-start = ((), (), s32[]{:S(2)}) async-start(), calls=%async_computation.5 | async-start | bytes 20971520 | tf_op jit(solution)/shard_map/reduce_scatter | solution.py:433
  292.0 32.4 %collective-permute-start.8 = (f32[4,1024,1024]{2,1,0:T(8,128)}, f32[4,1024,1024]{2,1,0:T(8,128)}, u32[]{:S(2)}, u32[]{:S(2)}) collective-permute-start(f32[4,1024,1024]{2,1,0:T(8,128)} %experts_forward.2), channel_id=1, source_target_pairs={{0,1},{1,0},{2,3},{3,2},{4,5},{5,4},{6,7},{7,6}} | collective-permute-start | bytes 50331656 | tf_op jit(solution)/shard_map/ppermute | solution.py:21
  462.9 81.6 %copy-start = (bf16[1024,1024]{1,0:T(8,128)(2,1)S(1)}, bf16[1024,1024]{1,0:T(8,128)(2,1)}, u32[]{:S(2)}) copy-start(bf16[1024,1024]{1,0:T(8,128)(2,1)} %get-tuple-element.84) | copy-start | bytes 6291460
Sparse Core Ops, SparseCore 0:
  9.8 92.5 all-gather.2
  104.8 85.2 all-gather.4
  244.7 148.8 reduce-scatter.2
  396.5 147.9 reduce-scatter.4
